TPU v7x, 128 devices: a whole 4x4x4 slice. The times are simulated.
128 devices in a mesh: gx: 16 (over z_hi, y, core), yz: 8 (over z_lo, x).
Axes of the slice: x: 4, y: 4, z: 4 (z_hi: 2, z_lo: 2; z = z_hi * 2 + z_lo), core: 2. Of those that a mesh axis runs over, the one named last changes fastest.
Arguments:
- spectra: bfloat16 [2, 20, 640, 32, 1024], P(None, None, None, 'gx', 'yz'), may hold values from -6 to 6
- kernel_mesh: float32 [20], replicated, may hold values from 0.02 to 6, as said below
- density: float32 [640, 32, 1024], P('gx', None, 'yz'), may hold values from 0.05 to 1
- local_wave: float32 [640, 32, 1024], P('gx', None, 'yz'), may hold values from 0.15 to 4.8
- wave_density: float32 [640, 32, 1024], P('gx', None, 'yz'), may hold values from -1.2 to 1.2
- wave_gradient: float32 [3, 640, 32, 1024], P(None, 'gx', None, 'yz'), may hold values from -0.6 to 0.6
Outputs:
- potential: float32 [640, 32, 1024], P('gx', None, 'yz')
Inputs may be any that keep to these rules, and one draw needn't show every extreme that they name: `kernel_mesh`: strictly increasing; entry 0 is at most 0.1 and entry 19 at least 5.0.
All inputs are finite; a program needn't handle non-finite values.
Results may differ from a plain program's by a relative error of at most 0.0033.
Values sent between devices are 32-bit elements.
No kernel may reach another device: no remote copies, remote signals or barrier semaphores. Data moves between devices by JAX's collectives and lax.ppermute only.
A program may use at most 192 MiB of HBM per device.

v0:
```python
import math

import jax
import jax.numpy as jnp
import numpy as np
from jax import lax
from jax.experimental import pallas as pl
from jax.experimental.pallas import tpu as pltpu
from jax.sharding import PartitionSpec as P

LANES = 128
COMPS_PER_STEP = 2
BLOCKS_PER_STEP = 2
IH, LOW, INV, MESH, ROWS = 0, 20, 40, 60, 80


def half_tables(length):
    half = length // 2
    cells = np.arange(half)[:, None]
    tables = []
    for parity in range(2):
        waves = 2 * np.arange(half)[None, :] + parity
        angles = 2.0 * math.pi * (waves * cells % length) / length
        tables.append(np.concatenate([np.cos(angles), -np.sin(angles)], axis=1))
    return np.stack(tables).astype(jnp.bfloat16)


def spline_table(mesh_ref, table_ref):
    points = mesh_ref.shape[0]
    tile = (8, LANES)
    mesh = [jnp.full(tile, mesh_ref[j], jnp.float32) for j in range(points)]
    steps = [mesh[j + 1] - mesh[j] for j in range(points - 1)]
    for j in range(points):
        table_ref[MESH + j] = mesh[j]
    for j in range(points - 1):
        table_ref[IH + j] = 1.0 / steps[j]
    low = jnp.zeros(tile, jnp.float32)
    for j in range(1, points - 1):
        pivot = (steps[j - 1] + steps[j]) / 3.0 - low * (steps[j - 1] / 6.0)
        inverse = 1.0 / pivot
        table_ref[LOW + j] = low
        table_ref[INV + j] = inverse
        low = (steps[j] / 6.0) * inverse
    table_ref[LOW + points - 1] = low


def transform_kernel(mesh_ref, tables_ref, spectra_ref, comp_ref, table_ref, scratch):
    @pl.when(pl.program_id(0) == 0)
    def _():
        spline_table(mesh_ref, table_ref)

    per_step = spectra_ref.shape[1]
    length = comp_ref.shape[2]
    half = length // 2
    for c in range(per_step):
        for p in range(2):
            scratch[c, p] = spectra_ref[p, c].astype(jnp.float32)
        parts = []
        for parity in range(2):
            operand = jnp.concatenate(
                [
                    jnp.concatenate(
                        [
                            scratch[c, p, pl.ds(2 * parity + y, half, stride=4), :].astype(jnp.bfloat16)
                            for y in range(2)
                        ],
                        axis=1,
                    )
                    for p in range(2)
                ],
                axis=0,
            )
            parts.append(jnp.dot(tables_ref[parity], operand, preferred_element_type=jnp.float32))
        total, difference = parts[0] + parts[1], parts[0] - parts[1]
        for y in range(2):
            comp_ref[c, y, :half, :] = total[:, y * LANES : (y + 1) * LANES]
            comp_ref[c, y, half:, :] = difference[:, y * LANES : (y + 1) * LANES]


def transform(spectra, kernel_mesh):
    comps, length = spectra.shape[1], spectra.shape[2]
    per_step = COMPS_PER_STEP
    tables = jnp.asarray(half_tables(length))
    flat = spectra.reshape(2, comps, 2 * length, LANES)
    return pl.pallas_call(
        transform_kernel,
        grid=(comps // per_step,),
        in_specs=[
            pl.BlockSpec(memory_space=pltpu.SMEM),
            pl.BlockSpec((2, length // 2, length), lambda i: (0, 0, 0)),
            pl.BlockSpec((2, per_step, 2 * length, LANES), lambda i: (0, i, 0, 0)),
        ],
        out_specs=[
            pl.BlockSpec((per_step, 2, length, LANES), lambda i: (i, 0, 0, 0)),
            pl.BlockSpec((ROWS, 8, LANES), lambda i: (0, 0, 0)),
        ],
        out_shape=[
            jax.ShapeDtypeStruct((comps, 2, length, LANES), jnp.float32),
            jax.ShapeDtypeStruct((ROWS, 8, LANES), jnp.float32),
        ],
        scratch_shapes=[pltpu.VMEM((per_step, 2, 2 * length, LANES), jnp.float32)],
        cost_estimate=pl.CostEstimate(
            flops=4 * comps * length * length * LANES,
            bytes_accessed=12 * comps * length * 2 * LANES,
            transcendentals=0,
        ),
        name="transform",
    )(kernel_mesh, tables, flat)


def evaluate(comp, table, wave):
    points = 20
    step, before = None, None
    forward = [None] * points
    for j in range(points - 1):
        step = (comp(j + 1) - comp(j)) * table(IH + j)
        if j >= 1:
            right = step - before
            forward[j] = right if j == 1 else right - table(LOW + j) * forward[j - 1]
        before = step
    second = [None] * points
    second[points - 1] = jnp.zeros_like(wave)
    second[0] = jnp.zeros_like(wave)
    for j in range(points - 2, 0, -1):
        second[j] = forward[j] * table(INV + j)
        if j < points - 2:
            second[j] = second[j] - table(LOW + j + 1) * second[j + 1]

    def pick(node):
        held = [node(points - 4 + i) for i in range(4)]
        for first in range(points - 7, 0, -3):
            below = wave < table(MESH + first + 3)
            held = [jnp.where(below, node(first + i), held[i]) for i in range(4)]
        below = wave < table(MESH + 1)
        return [jnp.where(below, node(min(i, 1)), held[i]) for i in range(4)]

    def ends(four, past_one, past_two):
        lower = jnp.where(past_two, four[2], jnp.where(past_one, four[1], four[0]))
        upper = jnp.where(past_two, four[3], jnp.where(past_one, four[2], four[1]))
        return lower, upper

    points_four = pick(lambda j: table(MESH + j))
    past_one, past_two = wave >= points_four[1], wave >= points_four[2]
    low, high = ends(points_four, past_one, past_two)
    comp_low, comp_high = ends(pick(comp), past_one, past_two)
    second_low, second_high = ends(pick(lambda j: second[j]), past_one, past_two)
    width = high - low
    inverse = 1.0 / width
    a = (high - wave) * inverse
    b = (wave - low) * inverse
    sixth = width * (1.0 / 6.0)
    a2, b2 = a * a, b * b
    value = a * comp_low + b * comp_high + (
        (a2 - 1.0) * a * second_low + (b2 - 1.0) * b * second_high
    ) * (width * sixth)
    slope = (comp_high - comp_low) * inverse + (
        (3.0 * b2 - 1.0) * second_high - (3.0 * a2 - 1.0) * second_low
    ) * sixth
    return value, slope


def spline_kernel(scale, table_ref, comp_ref, wave_ref, out_ref):
    blocks, width = wave_ref.shape[0], wave_ref.shape[2]
    count = out_ref.shape[0]
    tiles = width // 8
    step = pl.program_id(0)
    for k in range(blocks):
        block = step * blocks + k
        for y in range(2):
            value, slope = evaluate(
                lambda j: comp_ref[j, y, k * width : (k + 1) * width, :].reshape(tiles, 8, LANES),
                lambda j: table_ref[j],
                wave_ref[k, y].reshape(tiles, 8, LANES),
            )
            value = (value * scale).reshape(width, LANES)
            slope = (slope * scale).reshape(width, LANES)
            out_ref[block, y * width : (y + 1) * width, :] = value
            out_ref[block, (2 + y) * width : (3 + y) * width, :] = slope
            following = lax.rem(block + 1, count)
            previous = lax.rem(block + count - 1, count)
            out_ref[following, 4 * width + y : 4 * width + y + 1, :] = slope[width - 1 :]
            out_ref[previous, 4 * width + 2 + y : 4 * width + 3 + y, :] = slope[:1]
            out_ref[block, 4 * width + 4 + 2 * y : 4 * width + 6 + 2 * y, :] = slope[:2]


def splines(comp, table, wave):
    count, width = wave.shape[0], wave.shape[2]
    comps, length = comp.shape[0], comp.shape[2]
    blocks = BLOCKS_PER_STEP
    message = 4 * width + 8
    import functools

    return pl.pallas_call(
        functools.partial(spline_kernel, length ** (-0.5)),
        grid=(count // blocks,),
        in_specs=[
            pl.BlockSpec((ROWS, 8, LANES), lambda i: (0, 0, 0)),
            pl.BlockSpec((comps, 2, blocks * width, LANES), lambda i: (0, 0, i, 0)),
            pl.BlockSpec((blocks, 2, width, LANES), lambda i: (i, 0, 0, 0)),
        ],
        out_specs=pl.BlockSpec((count, message, LANES), lambda i: (0, 0, 0)),
        out_shape=jax.ShapeDtypeStruct((count, message, LANES), jnp.float32),
        name="splines",
    )(table, comp, wave)


def neighbours(axis):
    count = lax.axis_size(axis)
    forward = [(i, (i + 1) % count) for i in range(count)]
    return forward, [(target, source) for source, target in forward]


def shards(spectra, kernel_mesh, density, local_wave, wave_density, wave_gradient):
    width, rows = density.shape[0], density.shape[1]
    count = lax.axis_size("gx")
    wave = local_wave.reshape(width, count, 2, LANES).transpose(1, 2, 0, 3)
    wave = lax.all_to_all(wave, "gx", 0, 0, tiled=True)
    comp, table = transform(spectra, kernel_mesh)
    sent = splines(comp, table, wave)
    got = lax.all_to_all(sent, "gx", 0, 0, tiled=True)

    forward, backward = neighbours("gx")
    push = density * wave_gradient[0]
    push_low = lax.ppermute(push[-1:], "gx", forward)
    push_high = lax.ppermute(push[:1], "gx", backward)

    def field(at):
        part = got[:, at * width : (at + 2) * width].reshape(rows, width, LANES)
        return part.transpose(1, 0, 2)

    sum_value, sum_slope = field(0), field(2)
    edge = got[:, 4 * width : 4 * width + 4].reshape(count, 2, 2, LANES).transpose(1, 0, 2, 3)
    edge = edge.reshape(2, rows, LANES)
    local_term = sum_value + density * wave_density * sum_slope
    grad_scale = density * sum_slope
    flux_first = jnp.concatenate([push_low * edge[:1], push * sum_slope, push_high * edge[1:]], axis=0)
    flux_second = grad_scale * wave_gradient[1]
    flux_third = grad_scale * wave_gradient[2]
    forward, backward = neighbours("yz")
    third_low = lax.ppermute(flux_third[:, :, -1], "yz", forward)
    third_high = lax.ppermute(flux_third[:, :, 0], "yz", backward)
    padded = jnp.concatenate([third_low[:, :, None], flux_third, third_high[:, :, None]], axis=2)
    divergence = 0.5 * (flux_first[2:] - flux_first[:-2])
    divergence = divergence + 0.5 * (jnp.roll(flux_second, -1, 1) - jnp.roll(flux_second, 1, 1))
    divergence = divergence + 0.5 * (padded[:, :, 2:] - padded[:, :, :-2])
    return local_term - divergence


def solution(mesh):
    return jax.shard_map(
        shards,
        mesh=mesh,
        in_specs=(
            P(None, None, None, "gx", "yz"),
            P(),
            P("gx", None, "yz"),
            P("gx", None, "yz"),
            P("gx", None, "yz"),
            P(None, "gx", None, "yz"),
        ),
        out_specs=P("gx", None, "yz"),
        check_vma=False,
    )
```

profile of v0, /device:TPU:31, one launch (start us, length us, event | category | flops | bytes accessed | tf_op | source)
XLA Modules:
  0.0 87.6 jit_solution(2767824674156072246)
XLA Ops:
  0.0 2.3 %copy.34 = f32[40,32,128]{2,0,1:T(8,128)} copy(f32[40,32,128]{2,1,0:T(8,128)} %param.10) | data formatting | bytes 1310720 | tf_op args[3]
  2.3 8.3 %all-to-all-start = ((f32[16,2,40,128]{3,2,1,0:T(8,128)}), f32[16,2,40,128]{3,2,1,0:T(8,128)S(1)}, u32[]{:S(2)}, u32[]{:S(2)}) async-start(f32[16,2,40,128]{3,2,1,0:T(8,128)} %bitcast.2), calls=%async_computation | async-start | bytes 1310720 | tf_op jit(solution)/shard_map/all_to_all | solution.py:217
  10.6 15.6 %transform.1 = (f32[20,2,640,128]{3,2,1,0:T(8,128)}, f32[80,8,128]{2,1,0:T(8,128)}) custom-call(f32[20]{0:T(128)} %mesh_ref.1, bf16[2,320,640]{2,1,0:T(8,128)(2,1)} %constant.4.clone.tables_ref, bf16[2,20,1280,128]{3,2,1,0:T(8,128)(2,1)} %bitcast.48), custom_call_target="tpu_custom_call" | custom-call | flops 4194304000 | bytes 39321600 | tf_op jit(solution)/shard_map/transform/pallas_call | solution.py:85
  26.2 0.0 all-to-all-done.wave_ref
  26.2 0.0 copy-start.3
  26.2 0.8 copy-done.3
  27.1 11.3 %splines.1 = f32[16,168,128]{2,1,0:T(8,128)} custom-call(f32[80,8,128]{2,1,0:T(8,128)} %get-tuple-element.7.table_ref, f32[20,2,640,128]{3,2,1,0:T(8,128)} %get-tuple-element.8.comp_ref, f32[16,2,40,128]{3,2,1,0:T(8,128)} %copy-done.3), custom_call_target="tpu_custom_call" | custom-call | tf_op jit(solution)/shard_map/splines/pallas_call | solution.py:193
  38.4 26.5 %all_to_all.10 = f32[16,168,128]{2,1,0:T(8,128)S(1)} all-to-all(f32[16,168,128]{2,1,0:T(8,128)} %splines.1), channel_id=1, replica_groups=mesh['gx'=16,'yz'=8] {'gx'}, dimensions={0} | all-to-all | bytes 2752512 | tf_op jit(solution)/shard_map/all_to_all | solution.py:220
  64.8 0.0 copy-start.2
  64.8 0.0 copy-start.4
  64.8 0.1 fusion.7
  64.9 1.0 %copy-done.2 = f32[40,32,128]{2,1,0:T(8,128)S(1)} copy-done((f32[40,32,128]{2,1,0:T(8,128)S(1)}, f32[40,32,128]{2,1,0:T(8,128)}, u32[]{:S(2)}) %copy-start.2) | copy-done | bytes 655384
  65.9 0.7 copy-done.4
  66.6 1.2 %bitcast_multiply_fusion.4 = (f32[40,32,128]{2,1,0:T(8,128)}, f32[40,32,128]{2,1,0:T(8,128)S(1)}, f32[40,32,128]{2,1,0:T(8,128)S(1)}, f32[40,32,128]{2,1,0:T(8,128)S(1)}) fusion(f32[32,40,128]{2,1,0:T(8,128)S(1)} %bitcast.37, f32[40,32,128]{2,1,0:T(8,128)S(1)} %copy-done.2, f32[3,40,32,128]{3,2,1,0:T(8,128)S(1)} %copy-done.4), kind=kLoop, calls=%fused_computation.15 | loop fusion | flops 819200 | bytes 5898240 | tf_op jit(solution)/shard_map/mul | solution.py:236
  67.8 1.2 %fusion.9 = (f32[40,31,128]{2,1,0:T(8,128)}, f32[40,31,128]{2,1,0:T(8,128)}) fusion(f32[40,32,128]{2,1,0:T(8,128)S(1)} %get-tuple-element.11), kind=kLoop, calls=%fused_computation.21 | loop fusion | bytes 2539520 | tf_op jit(solution)/shard_map/jit(_roll_static)/slice | solution.py:244
  69.0 0.1 collective-permute-start
  69.1 5.3 %collective-permute-start.1 = (f32[1,32,128]{2,1,0:T(8,128)S(1)}, f32[1,32,128]{2,1,0:T(8,128)S(1)}, u32[]{:S(2)}, u32[]{:S(2)}) collective-permute-start(f32[1,32,128]{2,1,0:T(8,128)S(1)} %get-tuple-element.20), channel_id=1, source_target_pairs={{0,8},{8,16},{16,24},{24,32},{32,40},{40,48},{48,56},{56,64},{64,7... | collective-permute-start | bytes 49160 | tf_op jit(solution)/shard_map/ppermute | solution.py:224
  74.5 0.2 fusion.11
  74.7 0.4 copy.38
  75.1 0.0 copy-start
  75.1 0.4 copy.40
  75.5 0.7 collective-permute-start.3
  76.2 0.8 collective-permute-start.2
  77.1 3.9 %collective-permute-done.2 = f32[40,32]{0,1:T(8,128)S(1)} collective-permute-done((f32[40,32]{0,1:T(8,128)S(1)}, f32[40,32]{0,1:T(8,128)S(1)}, u32[]{:S(2)}, u32[]{:S(2)}) %collective-permute-start.2) | collective-permute-done | bytes 5152 | tf_op jit(solution)/shard_map/ppermute | solution.py:241
  80.9 1.4 %copy.39 = f32[40,32,1]{2,1,0:T(8,128)} copy(f32[40,32,1]{0,1,2:T(8,128)S(1)} %bitcast.47) | data formatting | bytes 10240 | tf_op jit(solution)/shard_map/broadcast_in_dim | solution.py:242
  82.3 0.0 collective-permute-done.3
  82.3 1.4 %copy.41 = f32[40,32,1]{2,1,0:T(8,128)} copy(f32[40,32,1]{0,1,2:T(8,128)S(1)} %bitcast.45) | data formatting | bytes 10240 | tf_op jit(solution)/shard_map/broadcast_in_dim | solution.py:242
  83.8 0.0 collective-permute-done
  83.8 0.0 collective-permute-done.1
  83.8 0.0 copy-done
  83.8 0.0 copy-done.1
  83.8 3.8 %fusion.3 = f32[40,32,128]{2,1,0:T(8,128)} fusion(f32[40,32,128]{2,1,0:T(8,128)S(1)} %get-tuple-element.12, f32[40,32,1]{2,1,0:T(8,128)} %copy.41, f32[40,32,1]{2,1,0:T(8,128)} %copy.39, f32[40,32,128]{2,1,0:T(8,128)} %get-tuple-element.9, f32[1,32,128]{2,1,0:T(8,128)S(1)} %mul.37, f32[1,32,128]{2,1,0:T(8,128)S(1)} %mul.36, ...), kind=kLoop, calls=%fused_computation.4 | loop fusion | flops 2621440 | bytes 5941248 | tf_op jit(solution)/shard_map/sub | solution.py:246
  (8 shorter events, 0.1 us)
Async XLA Ops:
  2.3 23.9 %all-to-all-start = ((f32[16,2,40,128]{3,2,1,0:T(8,128)}), f32[16,2,40,128]{3,2,1,0:T(8,128)S(1)}, u32[]{:S(2)}, u32[]{:S(2)}) async-start(f32[16,2,40,128]{3,2,1,0:T(8,128)} %bitcast.2), calls=%async_computation | async-start | bytes 1310720 | tf_op jit(solution)/shard_map/all_to_all | solution.py:217
  26.2 0.8 copy-start.3
  64.8 1.1 %copy-start.2 = (f32[40,32,128]{2,1,0:T(8,128)S(1)}, f32[40,32,128]{2,1,0:T(8,128)}, u32[]{:S(2)}) copy-start(f32[40,32,128]{2,1,0:T(8,128)} %param.9) | copy-start | bytes 1966084
  64.8 1.8 %copy-start.4 = (f32[3,40,32,128]{3,2,1,0:T(8,128)S(1)}, f32[3,40,32,128]{3,2,1,0:T(8,128)}, u32[]{:S(2)}) copy-start(f32[3,40,32,128]{3,2,1,0:T(8,128)} %param.12) | copy-start | bytes 5898244
  69.0 14.7 %collective-permute-start = (f32[1,32,128]{2,1,0:T(8,128)S(1)}, f32[1,32,128]{2,1,0:T(8,128)S(1)}, u32[]{:S(2)}, u32[]{:S(2)}) collective-permute-start(f32[1,32,128]{2,1,0:T(8,128)S(1)} %get-tuple-element.19), channel_id=1, source_target_pairs={{8,0},{16,8},{24,16},{32,24},{40,32},{48,40},{56,48},{64,56},{72,6... | collective-permute-start | bytes 49160 | tf_op jit(solution)/shard_map/ppermute | solution.py:225
  69.1 14.7 %collective-permute-start.1 = (f32[1,32,128]{2,1,0:T(8,128)S(1)}, f32[1,32,128]{2,1,0:T(8,128)S(1)}, u32[]{:S(2)}, u32[]{:S(2)}) collective-permute-start(f32[1,32,128]{2,1,0:T(8,128)S(1)} %get-tuple-element.20), channel_id=1, source_target_pairs={{0,8},{8,16},{16,24},{24,32},{32,40},{40,48},{48,56},{56,64},{64,7... | collective-permute-start | bytes 49160 | tf_op jit(solution)/shard_map/ppermute | solution.py:224
  75.1 8.7 %copy-start = (f32[40,31,128]{2,1,0:T(8,128)S(1)}, f32[40,31,128]{2,1,0:T(8,128)}, u32[]{:S(2)}) copy-start(f32[40,31,128]{2,1,0:T(8,128)} %get-tuple-element.17) | copy-start | bytes 1904644
  75.5 8.3 %copy-start.1 = (f32[40,31,128]{2,1,0:T(8,128)S(1)}, f32[40,31,128]{2,1,0:T(8,128)}, u32[]{:S(2)}) copy-start(f32[40,31,128]{2,1,0:T(8,128)} %get-tuple-element.18) | copy-start | bytes 1904644
  75.5 6.8 %collective-permute-start.3 = (f32[40,32]{0,1:T(8,128)S(1)}, f32[40,32]{0,1:T(8,128)S(1)}, u32[]{:S(2)}, u32[]{:S(2)}) collective-permute-start(f32[40,32]{0,1:T(8,128)S(1)} %bitcast.44), channel_id=1, source_target_pairs={{0,1},{1,2},{2,3},{3,4},{4,5},{5,6},{6,7},{7,0},{8,9},{9,10},{10,1... | collective-permute-start | bytes 15368 | tf_op jit(solution)/shard_map/ppermute | solution.py:240
  76.2 4.7 %collective-permute-start.2 = (f32[40,32]{0,1:T(8,128)S(1)}, f32[40,32]{0,1:T(8,128)S(1)}, u32[]{:S(2)}, u32[]{:S(2)}) collective-permute-start(f32[40,32]{0,1:T(8,128)S(1)} %bitcast.46), channel_id=1, source_target_pairs={{1,0},{2,1},{3,2},{4,3},{5,4},{6,5},{7,6},{0,7},{9,8},{10,9},{11,1... | collective-permute-start | bytes 15368 | tf_op jit(solution)/shard_map/ppermute | solution.py:241
where the time goes:
time: 88.3 us; the launch traced here: 87.6 us
  Pallas kernels  26.9 us (30%)
  blocking collectives  26.5 us (30%)
  starting transfers between devices  15.2 us (17%)
  local copies, waits for them, and re-layouts  10 us (11%)
  other arithmetic  5.06 us (6%)
  waiting for transfers between devices  3.89 us (4%)
    all_to_all x1, blocking collectives, shards(): got = lax.all_to_all(sent, 'gx', 0, 0, tiled=True)  26.5 us
    pallas_call x1, Pallas kernels, transform(): pl.pallas_call(transform_kernel, grid=(comps // per_step,), in_specs=[pl....  15.6 us
    pallas_call x1, Pallas kernels, splines(): pl.pallas_call(functools.partial(spline_kernel, length ** (-0.5)), grid=(...  11.3 us
    all_to_all x1, starting transfers between devices, shards(): wave = lax.all_to_all(wave, 'gx', 0, 0, tiled=True)  8.3 us
    ppermute x1, starting transfers between devices, shards(): push_low = lax.ppermute(push[-1:], 'gx', forward)  5.35 us
    unnamed x11, local copies, waits for them, and re-layouts  4.82 us
    ppermute x1, waiting for transfers between devices, shards(): third_high = lax.ppermute(flux_third[:, :, 0], 'yz', backward)  3.88 us
    sub x1, other arithmetic, shards(): return local_term - divergence  3.82 us
  transfers between devices with their start and end apart: 5, of which 1 were waited for; matrix products, arithmetic and copies ran while one was open for 4% of the time, Pallas kernels for 18%

commit v1 on v0

v1 whole, which is shorter than its diff:
```python
import functools
import math

import jax
import jax.numpy as jnp
import numpy as np
from jax import lax
from jax.experimental import pallas as pl
from jax.experimental.pallas import tpu as pltpu
from jax.sharding import PartitionSpec as P

LANES = 128
POINTS = 20
GROUP = 4
SLICES = 4
IH, LOW, INV, ROWS = 0, 20, 40, 60


def in_hbm(array):
    return pltpu.with_memory_space_constraint(array, pltpu.HBM)


def half_tables(length):
    half = length // 2
    cells = np.arange(half)[:, None]
    tables = []
    for parity in range(2):
        waves = 2 * np.arange(half)[None, :] + parity
        angles = 2.0 * math.pi * (waves * cells % length) / length
        tables.append(np.concatenate([np.cos(angles), -np.sin(angles)], axis=1))
    return np.stack(tables).astype(jnp.bfloat16)


def spline_table(mesh_ref, table_ref):
    tile = (8, LANES)
    mesh = [jnp.full(tile, mesh_ref[j], jnp.float32) for j in range(POINTS)]
    steps = [mesh[j + 1] - mesh[j] for j in range(POINTS - 1)]
    for j in range(POINTS - 1):
        table_ref[IH + j] = 1.0 / steps[j]
    low = jnp.zeros(tile, jnp.float32)
    for j in range(1, POINTS - 1):
        pivot = (steps[j - 1] + steps[j]) / 3.0 - low * (steps[j - 1] / 6.0)
        inverse = 1.0 / pivot
        table_ref[LOW + j] = low
        table_ref[INV + j] = inverse
        low = (steps[j] / 6.0) * inverse
    table_ref[LOW + POINTS - 1] = low


def transform_kernel(mesh_ref, tables_hbm, spectra_ref, comp_ref, table_out, tables_ref, held, wide, done, table_ref, arrived, left):
    length = comp_ref.shape[1]
    half = length // 2
    groups = POINTS // GROUP

    def copy(c):
        return pltpu.make_async_copy(spectra_ref.at[:, c], held.at[c], arrived.at[c])

    def store(g, slot):
        return pltpu.make_async_copy(done.at[slot], comp_ref.at[pl.ds(g * (2 * GROUP), 2 * GROUP)], left.at[slot])

    tables_copy = pltpu.make_async_copy(tables_hbm, tables_ref, left.at[3])
    copy(0).start()
    tables_copy.start()
    for c in range(1, POINTS):
        copy(c).start()
    spline_table(mesh_ref, table_ref)
    table_copy = pltpu.make_async_copy(table_ref, table_out, left.at[2])
    table_copy.start()
    tables_copy.wait()

    def group(g, carry):
        slot = lax.rem(g, 2)

        @pl.when(g >= 2)
        def _():
            store(g - 2, slot).wait()

        for i in range(GROUP):
            copy(g * GROUP + i).wait()
        for i in range(GROUP):
            c = g * GROUP + i
            for p in range(2):
                wide[i, p] = held[c, p].astype(jnp.float32)
            parts = []
            for parity in range(2):
                operand = jnp.concatenate(
                    [
                        jnp.concatenate(
                            [
                                wide[i, p, pl.ds(2 * parity + y, half, stride=4), :].astype(jnp.bfloat16)
                                for y in range(2)
                            ],
                            axis=1,
                        )
                        for p in range(2)
                    ],
                    axis=0,
                )
                parts.append(jnp.dot(tables_ref[parity], operand, preferred_element_type=jnp.float32))
            total, difference = parts[0] + parts[1], parts[0] - parts[1]
            for y in range(2):
                done[slot, 2 * i + y, :half, :] = total[:, y * LANES : (y + 1) * LANES]
                done[slot, 2 * i + y, half:, :] = difference[:, y * LANES : (y + 1) * LANES]
        store(g, slot).start()
        return carry

    lax.fori_loop(0, groups, group, 0)
    for g in range(groups - 2, groups):
        store(g, g % 2).wait()
    table_copy.wait()


def transform(spectra, kernel_mesh):
    comps, length = spectra.shape[1], spectra.shape[2]
    tables = jnp.asarray(half_tables(length))
    flat = spectra.reshape(2, comps, 2 * length, LANES)
    return pl.pallas_call(
        transform_kernel,
        in_specs=[
            pl.BlockSpec(memory_space=pltpu.SMEM),
            pl.BlockSpec(memory_space=pltpu.HBM),
            pl.BlockSpec(memory_space=pltpu.HBM),
        ],
        out_specs=[pl.BlockSpec(memory_space=pltpu.HBM), pl.BlockSpec(memory_space=pltpu.HBM)],
        out_shape=[
            pltpu.HBM((2 * comps, length, LANES), jnp.float32),
            pltpu.HBM((ROWS, 8, LANES), jnp.float32),
        ],
        scratch_shapes=[
            pltpu.VMEM((2, length // 2, length), jnp.bfloat16),
            pltpu.VMEM((comps, 2, 2 * length, LANES), jnp.bfloat16),
            pltpu.VMEM((GROUP, 2, 2 * length, LANES), jnp.float32),
            pltpu.VMEM((2, 2 * GROUP, length, LANES), jnp.float32),
            pltpu.VMEM((ROWS, 8, LANES), jnp.float32),
            pltpu.SemaphoreType.DMA((comps,)),
            pltpu.SemaphoreType.DMA((4,)),
        ],
        compiler_params=pltpu.CompilerParams(vmem_limit_bytes=40 * 1024 * 1024),
        cost_estimate=pl.CostEstimate(
            flops=4 * comps * length * length * LANES,
            bytes_accessed=12 * comps * length * 2 * LANES,
            transcendentals=0,
        ),
        name="transform",
    )(kernel_mesh, in_hbm(tables), in_hbm(flat))


def solve(comp, table):
    before = (comp(1) - comp(0)) * table(IH)
    forward = [None] * POINTS
    for j in range(1, POINTS - 1):
        step = (comp(j + 1) - comp(j)) * table(IH + j)
        forward[j] = step - before
        if j > 1:
            forward[j] = forward[j] - table(LOW + j) * forward[j - 1]
        before = step
    second = [None] * POINTS
    for j in range(POINTS - 2, 0, -1):
        second[j] = forward[j] * table(INV + j)
        if j < POINTS - 2:
            second[j] = second[j] - table(LOW + j + 1) * second[j + 1]
    second[0] = second[POINTS - 1] = jnp.zeros_like(before)
    return second


def evaluate(comp, second, mesh, wave):
    def pick(node):
        held = [node(POINTS - 4 + i) for i in range(4)]
        for first in range(POINTS - 7, 0, -3):
            below = wave < mesh(first + 3)
            held = [jnp.where(below, node(first + i), held[i]) for i in range(4)]
        below = wave < mesh(1)
        return [jnp.where(below, node(min(i, 1)), held[i]) for i in range(4)]

    def ends(four, past_one, past_two):
        lower = jnp.where(past_two, four[2], jnp.where(past_one, four[1], four[0]))
        upper = jnp.where(past_two, four[3], jnp.where(past_one, four[2], four[1]))
        return lower, upper

    points_four = pick(mesh)
    past_one, past_two = wave >= points_four[1], wave >= points_four[2]
    low, high = ends(points_four, past_one, past_two)
    comp_low, comp_high = ends(pick(comp), past_one, past_two)
    second_low, second_high = ends(pick(second), past_one, past_two)
    width = high - low
    inverse = 1.0 / width
    a = (high - wave) * inverse
    b = (wave - low) * inverse
    sixth = width * (1.0 / 6.0)
    a2, b2 = a * a, b * b
    value = a * comp_low + b * comp_high + (
        (a2 - 1.0) * a * second_low + (b2 - 1.0) * b * second_high
    ) * (width * sixth)
    slope = (comp_high - comp_low) * inverse + (
        (3.0 * b2 - 1.0) * second_high - (3.0 * a2 - 1.0) * second_low
    ) * sixth
    return value, slope


def spline_kernel(scale, mesh_ref, table_ref, wave_ref, comp_ref, out_hbm, order_ref, out_ref, held, arrived, left):
    count, width = wave_ref.shape[0], wave_ref.shape[2]
    tiles = width // 8
    part = 2 * width + 4

    def copy(block):
        rows = pl.ds(pl.multiple_of(block * width, 8), width)
        return pltpu.make_async_copy(comp_ref.at[:, rows], held.at[block], arrived.at[block])

    def store(block):
        return pltpu.make_async_copy(out_ref.at[block], out_hbm.at[block], left.at[block])

    for block in range(count):
        copy(block).start()
    order_ref[...] = jnp.zeros_like(order_ref)
    mesh = [jnp.full((8, LANES), mesh_ref[j], jnp.float32) for j in range(POINTS)]

    def body(block, carry):
        following = lax.rem(block + 1, count)
        previous = lax.rem(block + count - 1, count)
        copy(block).wait()
        slopes = []
        for y in range(2):
            wave = wave_ref[block, y].reshape(tiles, 8, LANES)
            comp = lambda j: held[block, 2 * j + y].reshape(tiles, 8, LANES)
            second = solve(comp, lambda j: table_ref[j])
            value, slope = evaluate(comp, lambda j: second[j], lambda j: mesh[j], wave)
            value = (value * scale).reshape(width, LANES)
            slope = (slope * scale).reshape(width, LANES)
            out_ref[block, y * part : y * part + width, :] = value
            out_ref[block, y * part + width : y * part + 2 * width, :] = slope
            at = y * part + 2 * width
            out_ref[following, at : at + 1, :] = slope[width - 1 :]
            out_ref[previous, at + 1 : at + 2, :] = slope[:1]
            slopes.append(slope)
        slopes.append(jnp.zeros((LANES - 2 * width, LANES), jnp.float32))
        turned = jnp.concatenate(slopes, axis=0).T
        for side, edge in enumerate((turned[:1], turned[LANES - 1 :])):
            out_ref[block, 2 * width + 2 + side : 2 * width + 3 + side, :] = edge
            at = part + 2 * width + 2 + side
            out_ref[block, at : at + 1, :] = pltpu.roll(edge, LANES - width, 1)

        @pl.when(block >= 2)
        def _():
            store(block - 1).start()

        return carry

    lax.fori_loop(0, count, body, 0)
    store(0).start()
    store(count - 1).start()
    for block in range(count):
        store(block).wait()


def splines(kernel_mesh, comp, table, wave):
    count, width = wave.shape[0], wave.shape[2]
    planes, length = comp.shape[0], comp.shape[1]
    vmem = pl.BlockSpec(memory_space=pltpu.VMEM)
    hbm = pl.BlockSpec(memory_space=pltpu.HBM)
    message = (count, 4 * width + 8, LANES)
    return pl.pallas_call(
        functools.partial(spline_kernel, length ** (-0.5)),
        in_specs=[pl.BlockSpec(memory_space=pltpu.SMEM), vmem, vmem, hbm],
        out_specs=[hbm, vmem],
        out_shape=[pltpu.HBM(message, jnp.float32), jax.ShapeDtypeStruct((8, LANES), jnp.float32)],
        scratch_shapes=[
            pltpu.VMEM(message, jnp.float32),
            pltpu.VMEM((count, planes, width, LANES), jnp.float32),
            pltpu.SemaphoreType.DMA((count,)),
            pltpu.SemaphoreType.DMA((count,)),
        ],
        compiler_params=pltpu.CompilerParams(vmem_limit_bytes=28 * 1024 * 1024),
        name="splines",
    )(kernel_mesh, table, wave, in_hbm(comp))


def edges_kernel(order_ref, density_ref, gradient_ref, push_ref, weight_ref, density, first, third, arrived):
    width, rows = density_ref.shape[0], density_ref.shape[1]
    copies = [
        pltpu.make_async_copy(density_ref, density, arrived.at[0]),
        pltpu.make_async_copy(gradient_ref.at[2], third, arrived.at[1]),
        pltpu.make_async_copy(gradient_ref.at[0, 0], first.at[0], arrived.at[2]),
        pltpu.make_async_copy(gradient_ref.at[0, width - 1], first.at[1], arrived.at[3]),
    ]
    for copy in copies:
        copy.start()
    for copy in copies:
        copy.wait()
    push_ref[0] = density[0] * first[0]
    push_ref[1] = density[width - 1] * first[1]
    lane = lax.broadcasted_iota(jnp.int32, (rows, LANES), 1)
    low = order_ref[:1] + jnp.zeros((rows, LANES), jnp.float32)
    high = low
    for x in range(width):
        product = density[x] * third[x]
        low = jnp.where(lane == x, product[:, :1], low)
        high = jnp.where(lane == x, product[:, LANES - 1 :], high)
    weight_ref[0] = low
    weight_ref[1] = high


def edges(order, density, gradient):
    rows = density.shape[1]
    vmem, hbm = pl.BlockSpec(memory_space=pltpu.VMEM), pl.BlockSpec(memory_space=pltpu.HBM)
    face = jax.ShapeDtypeStruct((2, rows, LANES), jnp.float32)
    return pl.pallas_call(
        edges_kernel,
        in_specs=[vmem, hbm, hbm],
        out_specs=[vmem, vmem],
        out_shape=[face, face],
        scratch_shapes=[
            pltpu.VMEM(density.shape, jnp.float32),
            pltpu.VMEM((2, rows, LANES), jnp.float32),
            pltpu.VMEM(density.shape, jnp.float32),
            pltpu.SemaphoreType.DMA((4,)),
        ],
        compiler_params=pltpu.CompilerParams(vmem_limit_bytes=8 * 1024 * 1024),
        name="edges",
    )(order, in_hbm(density), in_hbm(gradient))


def faces_kernel(width, got_ref, weight_ref, out_ref):
    part, rows = 2 * width + 4, weight_ref.shape[1]
    for side in range(2):
        out_ref[side] = got_ref[pl.ds(2 * width + 2 + side, rows, stride=part), :] * weight_ref[side]


def faces(got, weight, width):
    vmem = pl.BlockSpec(memory_space=pltpu.VMEM)
    return pl.pallas_call(
        functools.partial(faces_kernel, width),
        in_specs=[vmem, vmem],
        out_specs=vmem,
        out_shape=jax.ShapeDtypeStruct(weight.shape, jnp.float32),
        compiler_params=pltpu.CompilerParams(vmem_limit_bytes=8 * 1024 * 1024),
        name="faces",
    )(got, weight)


def inner_kernel(got_ref, push_ref, density_ref, rate_ref, gradient_ref, result, density, rate, gradient, arrived):
    width, rows = density_ref.shape[0], density_ref.shape[1]
    part = 2 * width + 4
    share = width // SLICES

    def copies(n):
        at = pl.ds(n * share, share)
        return [
            pltpu.make_async_copy(density_ref.at[at], density.at[at], arrived.at[n, 0]),
            pltpu.make_async_copy(rate_ref.at[at], rate.at[at], arrived.at[n, 1]),
            pltpu.make_async_copy(gradient_ref.at[:, at], gradient.at[:, at], arrived.at[n, 2]),
        ]

    for n in range(SLICES):
        for copy in copies(n):
            copy.start()

    def field(at):
        return got_ref[pl.ds(at, rows, stride=part), :]

    lane = lax.broadcasted_iota(jnp.int32, (rows, LANES), 1)
    ready = 0
    slope = [None] * width
    first = [None] * width
    for x in range(-1, width):
        ahead = x + 1
        if ahead < width:
            if ahead % share == 0:
                for copy in copies(ahead // share):
                    copy.wait()
            slope[ahead] = field(width + ahead) * density[ahead]
            first[ahead] = slope[ahead] * gradient[0, ahead]
        if x < 0:
            continue
        below = first[x - 1] if x > 0 else field(2 * width) * push_ref[0]
        above = first[x + 1] if x + 1 < width else field(2 * width + 1) * push_ref[1]
        second = slope[x] * gradient[1, x]
        third = slope[x] * gradient[2, x]
        beyond = jnp.where(lane == LANES - 1, 0.0, pltpu.roll(third, LANES - 1, 1))
        behind = jnp.where(lane == 0, 0.0, pltpu.roll(third, 1, 1))
        divergence = (above - below) + (beyond - behind)
        divergence = divergence + (pltpu.roll(second, rows - 1, 0) - pltpu.roll(second, 1, 0))
        result[x] = field(x) + rate[x] * slope[x] - 0.5 * divergence


def inner(got, push, density, rate, gradient):
    vmem, hbm = pl.BlockSpec(memory_space=pltpu.VMEM), pl.BlockSpec(memory_space=pltpu.HBM)
    return pl.pallas_call(
        inner_kernel,
        in_specs=[vmem, vmem, hbm, hbm, hbm],
        out_specs=vmem,
        out_shape=jax.ShapeDtypeStruct(density.shape, jnp.float32),
        scratch_shapes=[
            pltpu.VMEM(density.shape, jnp.float32),
            pltpu.VMEM(density.shape, jnp.float32),
            pltpu.VMEM(gradient.shape, jnp.float32),
            pltpu.SemaphoreType.DMA((SLICES, 3)),
        ],
        compiler_params=pltpu.CompilerParams(vmem_limit_bytes=16 * 1024 * 1024),
        name="inner",
    )(got, push, in_hbm(density), in_hbm(rate), in_hbm(gradient))


def outer_kernel(part_ref, low_ref, high_ref, out_hbm, out_ref, left):
    width, rows = part_ref.shape[0], part_ref.shape[1]
    share = width // SLICES
    lane = lax.broadcasted_iota(jnp.int32, (rows, LANES), 1)

    def store(n):
        at = pl.ds(n * share, share)
        return pltpu.make_async_copy(out_ref.at[at], out_hbm.at[at], left.at[n])

    for x in range(width):
        high = jnp.where(lane == LANES - 1, high_ref[:, x : x + 1], 0.0)
        flux = jnp.where(lane == 0, low_ref[:, x : x + 1], 0.0) - high
        out_ref[x] = part_ref[x] + 0.5 * flux
        if (x + 1) % share == 0:
            store(x // share).start()
    for n in range(SLICES):
        store(n).wait()


def outer(part, low, high):
    vmem, hbm = pl.BlockSpec(memory_space=pltpu.VMEM), pl.BlockSpec(memory_space=pltpu.HBM)
    return pl.pallas_call(
        outer_kernel,
        in_specs=[vmem] * 3,
        out_specs=hbm,
        out_shape=jax.ShapeDtypeStruct(part.shape, jnp.float32),
        scratch_shapes=[pltpu.VMEM(part.shape, jnp.float32), pltpu.SemaphoreType.DMA((SLICES,))],
        compiler_params=pltpu.CompilerParams(vmem_limit_bytes=8 * 1024 * 1024),
        name="outer",
    )(part, low, high)


def neighbours(axis):
    count = lax.axis_size(axis)
    forward = [(i, (i + 1) % count) for i in range(count)]
    return forward, [(target, source) for source, target in forward]


def shards(spectra, kernel_mesh, density, local_wave, wave_density, wave_gradient):
    width, rows = density.shape[0], density.shape[1]
    count = lax.axis_size("gx")
    wave = local_wave.reshape(width, count, 2, LANES).transpose(1, 2, 0, 3)
    wave = lax.all_to_all(wave, "gx", 0, 0, tiled=True)
    comp, table = transform(spectra, kernel_mesh)
    sent, order = splines(kernel_mesh, comp, table, wave)
    got = lax.all_to_all(sent, "gx", 0, 0, tiled=True).reshape(-1, LANES)

    push, weight = edges(order, density, wave_gradient)
    forward, backward = neighbours("gx")
    push = jnp.concatenate(
        [lax.ppermute(push[1:], "gx", forward), lax.ppermute(push[:1], "gx", backward)], axis=0
    )
    forward, backward = neighbours("yz")
    got = pltpu.with_memory_space_constraint(got, pltpu.VMEM)
    third = faces(got, weight, width)
    low = lax.ppermute(third[1], "yz", forward)
    high = lax.ppermute(third[0], "yz", backward)
    part = inner(got, push, density, wave_density, wave_gradient)
    return outer(part, low, high)


def solution(mesh):
    return jax.shard_map(
        shards,
        mesh=mesh,
        in_specs=(
            P(None, None, None, "gx", "yz"),
            P(),
            P("gx", None, "yz"),
            P("gx", None, "yz"),
            P("gx", None, "yz"),
            P(None, "gx", None, "yz"),
        ),
        out_specs=P("gx", None, "yz"),
        check_vma=False,
    )
```

time: 88.3 us -> 76.5 us (0.87)
  the two profiles are of different devices: /device:TPU:31 before, /device:TPU:0 now
where the time goes in v1:
time: 76.5 us; the launch traced here: 76.2 us
  Pallas kernels  30.9 us (40%)
  starting transfers between devices  23.9 us (31%)
  waiting for transfers between devices  17.9 us (23%)
  local copies, waits for them, and re-layouts  3.27 us (4%)
    all_to_all x1, waiting for transfers between devices, shards(): got = lax.all_to_all(sent, 'gx', 0, 0, tiled=True).reshape(-1, LANES)  14.3 us
    pallas_call x1, Pallas kernels, transform(): pl.pallas_call(transform_kernel, in_specs=[pl.BlockSpec(memory_space=pltp...  13.8 us
    pallas_call x1, Pallas kernels, splines(): pl.pallas_call(functools.partial(spline_kernel, length ** (-0.5)), in_spe...  11.9 us
    all_to_all x1, starting transfers between devices, shards(): wave = lax.all_to_all(wave, 'gx', 0, 0, tiled=True)  8 us
    all_to_all x1, starting transfers between devices, shards(): got = lax.all_to_all(sent, 'gx', 0, 0, tiled=True).reshape(-1, LANES)  7.23 us
    ppermute x1, starting transfers between devices, shards(): lax.ppermute(push[:1], 'gx', backward)  4.95 us
    ppermute x1, waiting for transfers between devices, shards(): low = lax.ppermute(third[1], 'yz', forward)  3.59 us
    ppermute x1, starting transfers between devices, shards(): high = lax.ppermute(third[0], 'yz', backward)  3.28 us
  transfers between devices with their start and end apart: 6, of which 2 were waited for; matrix products, arithmetic and copies ran while one was open for 0% of the time, Pallas kernels for 23%

profile of v1, /device:TPU:0, one launch (start us, length us, event | category | flops | bytes accessed | tf_op | source)
XLA Modules:
  0.0 76.2 jit_solution(11271413851830740376)
XLA Ops:
  0.0 0.0 copy-start.1
  0.0 2.3 %copy.8 = f32[40,32,128]{2,0,1:T(8,128)} copy(f32[40,32,128]{2,1,0:T(8,128)} %param.10) | data formatting | bytes 1310720 | tf_op args[3]
  2.3 8.0 %all-to-all-start = ((f32[16,2,40,128]{3,2,1,0:T(8,128)}), f32[16,2,40,128]{3,2,1,0:T(8,128)S(1)}, u32[]{:S(2)}, u32[]{:S(2)}) async-start(f32[16,2,40,128]{3,2,1,0:T(8,128)} %bitcast.2), calls=%async_computation | async-start | bytes 1310720 | tf_op jit(solution)/shard_map/all_to_all | solution.py:445
  10.3 0.0 copy-done.1
  10.3 13.8 %transform.1 = (f32[40,640,128]{2,1,0:T(8,128)}, f32[60,8,128]{2,1,0:T(8,128)}) custom-call(f32[20]{0:T(128)S(1)} %copy-done.1, bf16[2,320,640]{2,1,0:T(8,128)(2,1)} %constant.2.clone.tables_hbm, bf16[2,20,1280,128]{3,2,1,0:T(8,128)(2,1)} %bitcast.11), custom_call_target="tpu_custom_call" | custom-call | flops 4194304000 | bytes 39321600 | tf_op jit(solution)/shard_map/transform/pallas_call | solution.py:117
  24.1 0.0 all-to-all-done.wave_ref
  24.1 0.0 copy-start
  24.1 0.9 %copy-done = f32[60,8,128]{2,1,0:T(8,128)S(1)} copy-done((f32[60,8,128]{2,1,0:T(8,128)S(1)}, f32[60,8,128]{2,1,0:T(8,128)}, u32[]{:S(2)}) %copy-start) | copy-done | bytes 245784
  25.1 11.9 %splines.1 = (f32[16,168,128]{2,1,0:T(8,128)}, f32[8,128]{1,0:T(8,128)S(1)}) custom-call(f32[20]{0:T(128)S(1)} %copy-done.1, f32[60,8,128]{2,1,0:T(8,128)S(1)} %copy-done, f32[16,2,40,128]{3,2,1,0:T(8,128)S(1)} %all-to-all-done.wave_ref, f32[40,640,128]{2,1,0:T(8,128)} %get-tuple-element.12.comp_ref), custom_call_target="tpu_custom_call" | custom-call | tf_op jit(solution)/shard_map/splines/pallas_call | solution.py:261
  37.0 7.2 %all-to-all-start.1 = ((f32[16,168,128]{2,1,0:T(8,128)}), f32[16,168,128]{2,1,0:T(8,128)S(1)}, u32[]{:S(2)}, u32[]{:S(2)}) async-start(f32[16,168,128]{2,1,0:T(8,128)} %get-tuple-element.13), calls=%async_computation.1 | async-start | bytes 2752512 | tf_op jit(solution)/shard_map/all_to_all | solution.py:448
  44.2 1.9 %edges.1 = (f32[2,32,128]{2,1,0:T(8,128)S(1)}, f32[2,32,128]{2,1,0:T(8,128)S(1)}) custom-call(f32[8,128]{1,0:T(8,128)S(1)} %get-tuple-element.14.order_ref, f32[40,32,128]{2,1,0:T(8,128)} %density_ref.3, f32[3,40,32,128]{3,2,1,0:T(8,128)} %gradient_ref.3), custom_call_target="tpu_custom_call" | custom-call | tf_op jit(solution)/shard_map/edges/pallas_call | solution.py:306
  46.1 0.5 collective-permute-start
  46.6 5.0 %collective-permute-start.1 = (f32[1,32,128]{2,1,0:T(8,128)S(1)}, f32[1,32,128]{2,1,0:T(8,128)S(1)}, u32[]{:S(2)}, u32[]{:S(2)}) collective-permute-start(f32[1,32,128]{2,1,0:T(8,128)S(1)} %get-tuple-element.20), channel_id=1, source_target_pairs={{8,0},{16,8},{24,16},{32,24},{40,32},{48,40},{56,48},{64,56},{72,6... | collective-permute-start | bytes 49160 | tf_op jit(solution)/shard_map/ppermute | solution.py:453
  51.5 14.3 %all-to-all-done.1 = f32[16,168,128]{2,1,0:T(8,128)S(1)} async-done(((f32[16,168,128]{2,1,0:T(8,128)}), f32[16,168,128]{2,1,0:T(8,128)S(1)}, u32[]{:S(2)}, u32[]{:S(2)}) %all-to-all-start.1) | async-done | bytes 1376288 | tf_op jit(solution)/shard_map/all_to_all | solution.py:448
  65.9 3.3 %collective-permute-start.3 = (f32[32,128]{1,0:T(8,128)S(1)}, f32[32,128]{1,0:T(8,128)S(1)}, u32[]{:S(2)}, u32[]{:S(2)}) collective-permute-start(f32[32,128]{1,0:T(8,128)S(1)} %get-tuple-element.17), channel_id=1, source_target_pairs={{1,0},{2,1},{3,2},{4,3},{5,4},{6,5},{7,6},{0,7},{9,8},{10,9},{11,1... | collective-permute-start | bytes 49160 | tf_op jit(solution)/shard_map/ppermute | solution.py:459
  69.2 0.0 collective-permute-start.2
  69.2 0.0 collective-permute-done
  69.2 0.0 collective-permute-done.1
  69.2 2.2 %inner.1.part_ref = f32[40,32,128]{2,1,0:T(8,128)S(1)} custom-call(f32[2688,128]{1,0:T(8,128)S(1)} %bitcast.10, f32[2,32,128]{2,1,0:T(8,128)S(1)} %pad_maximum_fusion.push_ref, f32[40,32,128]{2,1,0:T(8,128)} %density_ref.3, f32[40,32,128]{2,1,0:T(8,128)} %rate_ref.1, f32[3,40,32,128]{3,2,1,0:T(8,128)} %gradient_ref.3), custom_call_target="tpu_custom_call" | custom-call | tf_op jit(solution)/shard_map/inner/pallas_call | solution.py:387
  71.4 0.0 collective-permute-done.3.high_ref
  71.4 3.6 %collective-permute-done.2.low_ref = f32[32,128]{1,0:T(8,128)S(1)} collective-permute-done((f32[32,128]{1,0:T(8,128)S(1)}, f32[32,128]{1,0:T(8,128)S(1)}, u32[]{:S(2)}, u32[]{:S(2)}) %collective-permute-start.2) | collective-permute-done | bytes 16416 | tf_op jit(solution)/shard_map/ppermute | solution.py:458
  75.0 1.2 %outer.1 = f32[40,32,128]{2,1,0:T(8,128)} custom-call(f32[40,32,128]{2,1,0:T(8,128)S(1)} %inner.1.part_ref, f32[32,128]{1,0:T(8,128)S(1)} %collective-permute-done.2.low_ref, f32[32,128]{1,0:T(8,128)S(1)} %collective-permute-done.3.high_ref), custom_call_target="tpu_custom_call" | custom-call | tf_op jit(solution)/shard_map/outer/pallas_call | solution.py:424
  (4 shorter events, 0.0 us)
Async XLA Ops:
  0.0 10.3 %copy-start.1 = (f32[20]{0:T(128)S(1)}, f32[20]{0:T(128)}, u32[]{:S(2)}) copy-start(f32[20]{0:T(128)} %mesh_ref.3) | copy-start | bytes 244
  2.3 21.8 %all-to-all-start = ((f32[16,2,40,128]{3,2,1,0:T(8,128)}), f32[16,2,40,128]{3,2,1,0:T(8,128)S(1)}, u32[]{:S(2)}, u32[]{:S(2)}) async-start(f32[16,2,40,128]{3,2,1,0:T(8,128)} %bitcast.2), calls=%async_computation | async-start | bytes 1310720 | tf_op jit(solution)/shard_map/all_to_all | solution.py:445
  24.1 0.9 %copy-start = (f32[60,8,128]{2,1,0:T(8,128)S(1)}, f32[60,8,128]{2,1,0:T(8,128)}, u32[]{:S(2)}) copy-start(f32[60,8,128]{2,1,0:T(8,128)} %get-tuple-element.11.table_ref) | copy-start | bytes 737284
  37.0 28.9 %all-to-all-start.1 = ((f32[16,168,128]{2,1,0:T(8,128)}), f32[16,168,128]{2,1,0:T(8,128)S(1)}, u32[]{:S(2)}, u32[]{:S(2)}) async-start(f32[16,168,128]{2,1,0:T(8,128)} %get-tuple-element.13), calls=%async_computation.1 | async-start | bytes 2752512 | tf_op jit(solution)/shard_map/all_to_all | solution.py:448
  46.1 23.1 %collective-permute-start = (f32[1,32,128]{2,1,0:T(8,128)S(1)}, f32[1,32,128]{2,1,0:T(8,128)S(1)}, u32[]{:S(2)}, u32[]{:S(2)}) collective-permute-start(f32[1,32,128]{2,1,0:T(8,128)S(1)} %get-tuple-element.19), channel_id=1, source_target_pairs={{0,8},{8,16},{16,24},{24,32},{32,40},{40,48},{48,56},{56,64},{64,7... | collective-permute-start | bytes 49160 | tf_op jit(solution)/shard_map/ppermute | solution.py:453
  46.6 22.6 %collective-permute-start.1 = (f32[1,32,128]{2,1,0:T(8,128)S(1)}, f32[1,32,128]{2,1,0:T(8,128)S(1)}, u32[]{:S(2)}, u32[]{:S(2)}) collective-permute-start(f32[1,32,128]{2,1,0:T(8,128)S(1)} %get-tuple-element.20), channel_id=1, source_target_pairs={{8,0},{16,8},{24,16},{32,24},{40,32},{48,40},{56,48},{64,56},{72,6... | collective-permute-start | bytes 49160 | tf_op jit(solution)/shard_map/ppermute | solution.py:453
  65.9 5.5 %collective-permute-start.3 = (f32[32,128]{1,0:T(8,128)S(1)}, f32[32,128]{1,0:T(8,128)S(1)}, u32[]{:S(2)}, u32[]{:S(2)}) collective-permute-start(f32[32,128]{1,0:T(8,128)S(1)} %get-tuple-element.17), channel_id=1, source_target_pairs={{1,0},{2,1},{3,2},{4,3},{5,4},{6,5},{7,6},{0,7},{9,8},{10,9},{11,1... | collective-permute-start | bytes 49160 | tf_op jit(solution)/shard_map/ppermute | solution.py:459
  69.2 5.8 %collective-permute-start.2 = (f32[32,128]{1,0:T(8,128)S(1)}, f32[32,128]{1,0:T(8,128)S(1)}, u32[]{:S(2)}, u32[]{:S(2)}) collective-permute-start(f32[32,128]{1,0:T(8,128)S(1)} %get-tuple-element.18), channel_id=1, source_target_pairs={{0,1},{1,2},{2,3},{3,4},{4,5},{5,6},{6,7},{7,0},{8,9},{9,10},{10,1... | collective-permute-start | bytes 49160 | tf_op jit(solution)/shard_map/ppermute | solution.py:458

commit v2 on v1

--- a/solution.py
+++ b/solution.py
@@ -13,6 +13,8 @@
 POINTS = 20
 GROUP = 4
 SLICES = 4
+AHEAD = 8
+BLOCKS_AHEAD = 4
 IH, LOW, INV, ROWS = 0, 20, 40, 60
 
 
@@ -47,7 +49,7 @@
     table_ref[LOW + POINTS - 1] = low
 
 
-def transform_kernel(mesh_ref, tables_hbm, spectra_ref, comp_ref, table_out, tables_ref, held, wide, done, table_ref, arrived, left):
+def transform_kernel(mesh_ref, tables_hbm, spectra_ref, comp_ref, table_ref, tables_ref, held, wide, done, arrived, left):
     length = comp_ref.shape[1]
     half = length // 2
     groups = POINTS // GROUP
@@ -58,14 +60,12 @@
     def store(g, slot):
         return pltpu.make_async_copy(done.at[slot], comp_ref.at[pl.ds(g * (2 * GROUP), 2 * GROUP)], left.at[slot])
 
-    tables_copy = pltpu.make_async_copy(tables_hbm, tables_ref, left.at[3])
+    tables_copy = pltpu.make_async_copy(tables_hbm, tables_ref, left.at[2])
     copy(0).start()
     tables_copy.start()
-    for c in range(1, POINTS):
+    for c in range(1, AHEAD):
         copy(c).start()
     spline_table(mesh_ref, table_ref)
-    table_copy = pltpu.make_async_copy(table_ref, table_out, left.at[2])
-    table_copy.start()
     tables_copy.wait()
 
     def group(g, carry):
@@ -76,7 +76,13 @@
             store(g - 2, slot).wait()
 
         for i in range(GROUP):
-            copy(g * GROUP + i).wait()
+            c = g * GROUP + i
+            copy(c).wait()
+
+            @pl.when(c + AHEAD < POINTS)
+            def _():
+                copy(c + AHEAD).start()
+
         for i in range(GROUP):
             c = g * GROUP + i
             for p in range(2):
@@ -107,7 +113,6 @@
     lax.fori_loop(0, groups, group, 0)
     for g in range(groups - 2, groups):
         store(g, g % 2).wait()
-    table_copy.wait()
 
 
 def transform(spectra, kernel_mesh):
@@ -121,19 +126,18 @@
             pl.BlockSpec(memory_space=pltpu.HBM),
             pl.BlockSpec(memory_space=pltpu.HBM),
         ],
-        out_specs=[pl.BlockSpec(memory_space=pltpu.HBM), pl.BlockSpec(memory_space=pltpu.HBM)],
+        out_specs=[pl.BlockSpec(memory_space=pltpu.HBM), pl.BlockSpec(memory_space=pltpu.VMEM)],
         out_shape=[
             pltpu.HBM((2 * comps, length, LANES), jnp.float32),
-            pltpu.HBM((ROWS, 8, LANES), jnp.float32),
+            jax.ShapeDtypeStruct((ROWS, 8, LANES), jnp.float32),
         ],
         scratch_shapes=[
             pltpu.VMEM((2, length // 2, length), jnp.bfloat16),
             pltpu.VMEM((comps, 2, 2 * length, LANES), jnp.bfloat16),
             pltpu.VMEM((GROUP, 2, 2 * length, LANES), jnp.float32),
             pltpu.VMEM((2, 2 * GROUP, length, LANES), jnp.float32),
-            pltpu.VMEM((ROWS, 8, LANES), jnp.float32),
             pltpu.SemaphoreType.DMA((comps,)),
-            pltpu.SemaphoreType.DMA((4,)),
+            pltpu.SemaphoreType.DMA((3,)),
         ],
         compiler_params=pltpu.CompilerParams(vmem_limit_bytes=40 * 1024 * 1024),
         cost_estimate=pl.CostEstimate(
@@ -209,16 +213,31 @@
     def store(block):
         return pltpu.make_async_copy(out_ref.at[block], out_hbm.at[block], left.at[block])
 
-    for block in range(count):
+    for block in range(BLOCKS_AHEAD):
         copy(block).start()
     order_ref[...] = jnp.zeros_like(order_ref)
+    out_ref[count - 1] = jnp.zeros(out_ref.shape[1:], jnp.float32)
     mesh = [jnp.full((8, LANES), mesh_ref[j], jnp.float32) for j in range(POINTS)]
+
+    def turn(block):
+        slopes = [out_ref[block, y * part + width : y * part + 2 * width, :] for y in range(2)]
+        slopes.append(jnp.zeros((LANES - 2 * width, LANES), jnp.float32))
+        turned = jnp.concatenate(slopes, axis=0).T
+        for side, edge in enumerate((turned[:1], turned[LANES - 1 :])):
+            at = 2 * width + 2 + side
+            out_ref[block, at : at + 1, :] = edge
+            out_ref[block, part + at : part + at + 1, :] = pltpu.roll(edge, LANES - width, 1)
 
     def body(block, carry):
         following = lax.rem(block + 1, count)
         previous = lax.rem(block + count - 1, count)
         copy(block).wait()
-        slopes = []
+
+        @pl.when(block + BLOCKS_AHEAD < count)
+        def _():
+            copy(block + BLOCKS_AHEAD).start()
+
+        turn(previous)
         for y in range(2):
             wave = wave_ref[block, y].reshape(tiles, 8, LANES)
             comp = lambda j: held[block, 2 * j + y].reshape(tiles, 8, LANES)
@@ -231,14 +250,6 @@
             at = y * part + 2 * width
             out_ref[following, at : at + 1, :] = slope[width - 1 :]
             out_ref[previous, at + 1 : at + 2, :] = slope[:1]
-            slopes.append(slope)
-        slopes.append(jnp.zeros((LANES - 2 * width, LANES), jnp.float32))
-        turned = jnp.concatenate(slopes, axis=0).T
-        for side, edge in enumerate((turned[:1], turned[LANES - 1 :])):
-            out_ref[block, 2 * width + 2 + side : 2 * width + 3 + side, :] = edge
-            at = part + 2 * width + 2 + side
-            out_ref[block, at : at + 1, :] = pltpu.roll(edge, LANES - width, 1)
-
         @pl.when(block >= 2)
         def _():
             store(block - 1).start()
@@ -246,6 +257,7 @@
         return carry
 
     lax.fori_loop(0, count, body, 0)
+    turn(count - 1)
     store(0).start()
     store(count - 1).start()
     for block in range(count):
@@ -319,10 +331,10 @@
     )(order, in_hbm(density), in_hbm(gradient))
 
 
-def faces_kernel(width, got_ref, weight_ref, out_ref):
+def faces_kernel(width, got_ref, weight_ref, low_ref, high_ref):
     part, rows = 2 * width + 4, weight_ref.shape[1]
-    for side in range(2):
-        out_ref[side] = got_ref[pl.ds(2 * width + 2 + side, rows, stride=part), :] * weight_ref[side]
+    for side, out_ref in enumerate((low_ref, high_ref)):
+        out_ref[...] = got_ref[pl.ds(2 * width + 2 + side, rows, stride=part), :] * weight_ref[side]
 
 
 def faces(got, weight, width):
@@ -330,8 +342,8 @@
     return pl.pallas_call(
         functools.partial(faces_kernel, width),
         in_specs=[vmem, vmem],
-        out_specs=vmem,
-        out_shape=jax.ShapeDtypeStruct(weight.shape, jnp.float32),
+        out_specs=[vmem, vmem],
+        out_shape=[jax.ShapeDtypeStruct(weight.shape[1:], jnp.float32)] * 2,
         compiler_params=pltpu.CompilerParams(vmem_limit_bytes=8 * 1024 * 1024),
         name="faces",
     )(got, weight)
@@ -438,10 +450,39 @@
     return forward, [(target, source) for source, target in forward]
 
 
+def turn_kernel(wave_ref, out_ref, held, arrived):
+    width, rows = wave_ref.shape[0], wave_ref.shape[1]
+    share = width // SLICES
+
+    def copy(n):
+        at = pl.ds(n * share, share)
+        return pltpu.make_async_copy(wave_ref.at[at], held.at[at], arrived.at[n])
+
+    for n in range(SLICES):
+        copy(n).start()
+    for x in range(width):
+        if x % share == 0:
+            copy(x // share).wait()
+        out_ref[pl.ds(x, rows, stride=width), :] = held[x]
+
+
+def turn(wave):
+    width, rows = wave.shape[0], wave.shape[1]
+    return pl.pallas_call(
+        turn_kernel,
+        in_specs=[pl.BlockSpec(memory_space=pltpu.HBM)],
+        out_specs=pl.BlockSpec(memory_space=pltpu.VMEM),
+        out_shape=jax.ShapeDtypeStruct((rows * width, LANES), jnp.float32),
+        scratch_shapes=[pltpu.VMEM(wave.shape, jnp.float32), pltpu.SemaphoreType.DMA((SLICES,))],
+        compiler_params=pltpu.CompilerParams(vmem_limit_bytes=8 * 1024 * 1024),
+        name="turn",
+    )(in_hbm(wave))
+
+
 def shards(spectra, kernel_mesh, density, local_wave, wave_density, wave_gradient):
     width, rows = density.shape[0], density.shape[1]
     count = lax.axis_size("gx")
-    wave = local_wave.reshape(width, count, 2, LANES).transpose(1, 2, 0, 3)
+    wave = turn(local_wave).reshape(count, 2, width, LANES)
     wave = lax.all_to_all(wave, "gx", 0, 0, tiled=True)
     comp, table = transform(spectra, kernel_mesh)
     sent, order = splines(kernel_mesh, comp, table, wave)
@@ -454,9 +495,9 @@
     )
     forward, backward = neighbours("yz")
     got = pltpu.with_memory_space_constraint(got, pltpu.VMEM)
-    third = faces(got, weight, width)
-    low = lax.ppermute(third[1], "yz", forward)
-    high = lax.ppermute(third[0], "yz", backward)
+    third_low, third_high = faces(got, weight, width)
+    low = lax.ppermute(third_high, "yz", forward)
+    high = lax.ppermute(third_low, "yz", backward)
     part = inner(got, push, density, wave_density, wave_gradient)
     return outer(part, low, high)
 

time: 76.5 us -> 69.9 us (0.914)
  local copies, waits for them, and re-layouts: 3.27 us -> 0.01 us
  waiting for transfers between devices: 17.9 us -> 15.4 us
  Pallas kernels: 30.9 us -> 30 us
    ppermute x2, waiting for transfers between devices: 3.59 us -> 0.01 us  [the longest x1 0.01 us: shards(): high = lax.ppermute(third_low, 'yz', backward)]
    unnamed x5 -> x2, local copies, waits for them, and re-layouts: 3.26 us -> 0.01 us
    pallas_call x0 -> x1, Pallas kernels: none -> 2.06 us  [turn(): pl.pallas_call(turn_kernel, in_specs=[pl.BlockSpec(memory_space=pltpu.HBM...]
    pallas_call x1, Pallas kernels: 11.9 us -> 9.99 us  [splines(): pl.pallas_call(functools.partial(spline_kernel, length ** (-0.5)), in_spe...]
    pallas_call x1, Pallas kernels: 13.8 us -> 12.7 us  [transform(): pl.pallas_call(transform_kernel, in_specs=[pl.BlockSpec(memory_space=pltp...]
    all_to_all x1, waiting for transfers between devices: 0.01 us -> 1.06 us  [shards(): wave = lax.all_to_all(wave, 'gx', 0, 0, tiled=True)]
    all_to_all x1, starting transfers between devices: 7.23 us -> 6.18 us  [shards(): got = lax.all_to_all(sent, 'gx', 0, 0, tiled=True).reshape(-1, LANES)]
    ppermute x2, starting transfers between devices: 3.28 us -> 4.14 us  [the longest x1 2.64 us: shards(): high = lax.ppermute(third_low, 'yz', backward)]
  transfers between devices with their start and end apart: 6 -> 6, of which waited for: 2 -> 2; matrix products, arithmetic and copies ran while one was open for 0% -> 0% of each run, Pallas kernels for 23% -> 24%
where the time goes in v2:
time: 69.9 us; the launch traced here: 69.2 us
  Pallas kernels  30 us (43%)
  starting transfers between devices  23.8 us (34%)
  waiting for transfers between devices  15.4 us (22%)
    all_to_all x1, waiting for transfers between devices, shards(): got = lax.all_to_all(sent, 'gx', 0, 0, tiled=True).reshape(-1, LANES)  14.3 us
    pallas_call x1, Pallas kernels, transform(): pl.pallas_call(transform_kernel, in_specs=[pl.BlockSpec(memory_space=pltp...  12.7 us
    pallas_call x1, Pallas kernels, splines(): pl.pallas_call(functools.partial(spline_kernel, length ** (-0.5)), in_spe...  9.99 us
    all_to_all x1, starting transfers between devices, shards(): wave = lax.all_to_all(wave, 'gx', 0, 0, tiled=True)  8.01 us
    all_to_all x1, starting transfers between devices, shards(): got = lax.all_to_all(sent, 'gx', 0, 0, tiled=True).reshape(-1, LANES)  6.18 us
    ppermute x1, starting transfers between devices, shards(): lax.ppermute(push[:1], 'gx', backward)  4.95 us
    ppermute x1, starting transfers between devices, shards(): high = lax.ppermute(third_low, 'yz', backward)  2.64 us
    pallas_call x1, Pallas kernels, inner(): pl.pallas_call(inner_kernel, in_specs=[vmem, vmem, hbm, hbm, hbm], out_sp...  2.21 us
  transfers between devices with their start and end apart: 6, of which 2 were waited for; matrix products, arithmetic and copies ran while one was open for 0% of the time, Pallas kernels for 24%

profile of v2, /device:TPU:0, one launch (start us, length us, event | category | flops | bytes accessed | tf_op | source)
XLA Modules:
  0.0 69.2 jit_solution(5632536187972439661)
XLA Ops:
  0.0 0.0 copy-start
  0.0 2.1 %turn.1 = f32[1280,128]{1,0:T(8,128)} custom-call(f32[40,32,128]{2,1,0:T(8,128)} %wave_ref.1), custom_call_target="tpu_custom_call" | custom-call | tf_op jit(solution)/shard_map/turn/pallas_call | solution.py:471
  2.1 8.0 %all-to-all-start = ((f32[16,2,40,128]{3,2,1,0:T(8,128)}), f32[16,2,40,128]{3,2,1,0:T(8,128)S(1)}, u32[]{:S(2)}, u32[]{:S(2)}) async-start(f32[16,2,40,128]{3,2,1,0:T(8,128)} %bitcast.1), calls=%async_computation | async-start | bytes 1310720 | tf_op jit(solution)/shard_map/all_to_all | solution.py:486
  10.1 0.0 copy-done
  10.1 12.7 %transform.1 = (f32[40,640,128]{2,1,0:T(8,128)}, f32[60,8,128]{2,1,0:T(8,128)S(1)}) custom-call(f32[20]{0:T(128)S(1)} %copy-done, bf16[2,320,640]{2,1,0:T(8,128)(2,1)} %constant.2.clone.tables_hbm, bf16[2,20,1280,128]{3,2,1,0:T(8,128)(2,1)} %bitcast.5), custom_call_target="tpu_custom_call" | custom-call | flops 4194304000 | bytes 39321600 | tf_op jit(solution)/shard_map/transform/pallas_call | solution.py:122
  22.8 1.1 %all-to-all-done.wave_ref = f32[16,2,40,128]{3,2,1,0:T(8,128)S(1)} async-done(((f32[16,2,40,128]{3,2,1,0:T(8,128)}), f32[16,2,40,128]{3,2,1,0:T(8,128)S(1)}, u32[]{:S(2)}, u32[]{:S(2)}) %all-to-all-start) | async-done | bytes 655392 | tf_op jit(solution)/shard_map/all_to_all | solution.py:486
  23.8 10.0 %splines.1 = (f32[16,168,128]{2,1,0:T(8,128)}, f32[8,128]{1,0:T(8,128)S(1)}) custom-call(f32[20]{0:T(128)S(1)} %copy-done, f32[60,8,128]{2,1,0:T(8,128)S(1)} %get-tuple-element.13.table_ref, f32[16,2,40,128]{3,2,1,0:T(8,128)S(1)} %all-to-all-done.wave_ref, f32[40,640,128]{2,1,0:T(8,128)} %get-tuple-element.14.comp_ref), custom_call_target="tpu_custom_call" | custom-call | tf_op jit(solution)/shard_map/splines/pallas_call | solution.py:273
  33.8 6.2 %all-to-all-start.1 = ((f32[16,168,128]{2,1,0:T(8,128)}), f32[16,168,128]{2,1,0:T(8,128)S(1)}, u32[]{:S(2)}, u32[]{:S(2)}) async-start(f32[16,168,128]{2,1,0:T(8,128)} %get-tuple-element.15), calls=%async_computation.1 | async-start | bytes 2752512 | tf_op jit(solution)/shard_map/all_to_all | solution.py:489
  40.0 1.9 %edges.1 = (f32[2,32,128]{2,1,0:T(8,128)S(1)}, f32[2,32,128]{2,1,0:T(8,128)S(1)}) custom-call(f32[8,128]{1,0:T(8,128)S(1)} %get-tuple-element.16.order_ref, f32[40,32,128]{2,1,0:T(8,128)} %density_ref.3, f32[3,40,32,128]{3,2,1,0:T(8,128)} %gradient_ref.3), custom_call_target="tpu_custom_call" | custom-call | tf_op jit(solution)/shard_map/edges/pallas_call | solution.py:318
  41.9 0.5 collective-permute-start
  42.4 5.0 %collective-permute-start.1 = (f32[1,32,128]{2,1,0:T(8,128)S(1)}, f32[1,32,128]{2,1,0:T(8,128)S(1)}, u32[]{:S(2)}, u32[]{:S(2)}) collective-permute-start(f32[1,32,128]{2,1,0:T(8,128)S(1)} %get-tuple-element.22), channel_id=1, source_target_pairs={{8,0},{16,8},{24,16},{32,24},{40,32},{48,40},{56,48},{64,56},{72,6... | collective-permute-start | bytes 49160 | tf_op jit(solution)/shard_map/ppermute | solution.py:494
  47.3 14.3 %all-to-all-done.1 = f32[16,168,128]{2,1,0:T(8,128)S(1)} async-done(((f32[16,168,128]{2,1,0:T(8,128)}), f32[16,168,128]{2,1,0:T(8,128)S(1)}, u32[]{:S(2)}, u32[]{:S(2)}) %all-to-all-start.1) | async-done | bytes 1376288 | tf_op jit(solution)/shard_map/all_to_all | solution.py:489
  61.7 1.5 %collective-permute-start.2 = (f32[32,128]{1,0:T(8,128)S(1)}, f32[32,128]{1,0:T(8,128)S(1)}, u32[]{:S(2)}, u32[]{:S(2)}) collective-permute-start(f32[32,128]{1,0:T(8,128)S(1)} %get-tuple-element.19), channel_id=1, source_target_pairs={{0,1},{1,2},{2,3},{3,4},{4,5},{5,6},{6,7},{7,0},{8,9},{9,10},{10,1... | collective-permute-start | bytes 49160 | tf_op jit(solution)/shard_map/ppermute | solution.py:499
  63.2 2.6 %collective-permute-start.3 = (f32[32,128]{1,0:T(8,128)S(1)}, f32[32,128]{1,0:T(8,128)S(1)}, u32[]{:S(2)}, u32[]{:S(2)}) collective-permute-start(f32[32,128]{1,0:T(8,128)S(1)} %get-tuple-element.20), channel_id=1, source_target_pairs={{1,0},{2,1},{3,2},{4,3},{5,4},{6,5},{7,6},{0,7},{9,8},{10,9},{11,1... | collective-permute-start | bytes 49160 | tf_op jit(solution)/shard_map/ppermute | solution.py:500
  65.8 0.0 collective-permute-done
  65.8 0.0 collective-permute-done.1
  65.8 2.2 %inner.1.part_ref = f32[40,32,128]{2,1,0:T(8,128)S(1)} custom-call(f32[2688,128]{1,0:T(8,128)S(1)} %bitcast.4, f32[2,32,128]{2,1,0:T(8,128)S(1)} %pad_maximum_fusion.push_ref, f32[40,32,128]{2,1,0:T(8,128)} %density_ref.3, f32[40,32,128]{2,1,0:T(8,128)} %rate_ref.1, f32[3,40,32,128]{3,2,1,0:T(8,128)} %gradient_ref.3), custom_call_target="tpu_custom_call" | custom-call | tf_op jit(solution)/shard_map/inner/pallas_call | solution.py:399
  68.0 0.0 collective-permute-done.2.low_ref
  68.0 0.0 collective-permute-done.3.high_ref
  68.1 1.2 %outer.1 = f32[40,32,128]{2,1,0:T(8,128)} custom-call(f32[40,32,128]{2,1,0:T(8,128)S(1)} %inner.1.part_ref, f32[32,128]{1,0:T(8,128)S(1)} %collective-permute-done.2.low_ref, f32[32,128]{1,0:T(8,128)S(1)} %collective-permute-done.3.high_ref), custom_call_target="tpu_custom_call" | custom-call | tf_op jit(solution)/shard_map/outer/pallas_call | solution.py:436
  (3 shorter events, 0.0 us)
Async XLA Ops:
  0.0 10.1 %copy-start = (f32[20]{0:T(128)S(1)}, f32[20]{0:T(128)}, u32[]{:S(2)}) copy-start(f32[20]{0:T(128)} %mesh_ref.3) | copy-start | bytes 244
  2.1 21.8 %all-to-all-start = ((f32[16,2,40,128]{3,2,1,0:T(8,128)}), f32[16,2,40,128]{3,2,1,0:T(8,128)S(1)}, u32[]{:S(2)}, u32[]{:S(2)}) async-start(f32[16,2,40,128]{3,2,1,0:T(8,128)} %bitcast.1), calls=%async_computation | async-start | bytes 1310720 | tf_op jit(solution)/shard_map/all_to_all | solution.py:486
  33.8 27.8 %all-to-all-start.1 = ((f32[16,168,128]{2,1,0:T(8,128)}), f32[16,168,128]{2,1,0:T(8,128)S(1)}, u32[]{:S(2)}, u32[]{:S(2)}) async-start(f32[16,168,128]{2,1,0:T(8,128)} %get-tuple-element.15), calls=%async_computation.1 | async-start | bytes 2752512 | tf_op jit(solution)/shard_map/all_to_all | solution.py:489
  41.9 23.9 %collective-permute-start = (f32[1,32,128]{2,1,0:T(8,128)S(1)}, f32[1,32,128]{2,1,0:T(8,128)S(1)}, u32[]{:S(2)}, u32[]{:S(2)}) collective-permute-start(f32[1,32,128]{2,1,0:T(8,128)S(1)} %get-tuple-element.21), channel_id=1, source_target_pairs={{0,8},{8,16},{16,24},{24,32},{32,40},{40,48},{48,56},{56,64},{64,7... | collective-permute-start | bytes 49160 | tf_op jit(solution)/shard_map/ppermute | solution.py:494
  42.4 23.4 %collective-permute-start.1 = (f32[1,32,128]{2,1,0:T(8,128)S(1)}, f32[1,32,128]{2,1,0:T(8,128)S(1)}, u32[]{:S(2)}, u32[]{:S(2)}) collective-permute-start(f32[1,32,128]{2,1,0:T(8,128)S(1)} %get-tuple-element.22), channel_id=1, source_target_pairs={{8,0},{16,8},{24,16},{32,24},{40,32},{48,40},{56,48},{64,56},{72,6... | collective-permute-start | bytes 49160 | tf_op jit(solution)/shard_map/ppermute | solution.py:494
  61.7 6.4 %collective-permute-start.2 = (f32[32,128]{1,0:T(8,128)S(1)}, f32[32,128]{1,0:T(8,128)S(1)}, u32[]{:S(2)}, u32[]{:S(2)}) collective-permute-start(f32[32,128]{1,0:T(8,128)S(1)} %get-tuple-element.19), channel_id=1, source_target_pairs={{0,1},{1,2},{2,3},{3,4},{4,5},{5,6},{6,7},{7,0},{8,9},{9,10},{10,1... | collective-permute-start | bytes 49160 | tf_op jit(solution)/shard_map/ppermute | solution.py:499
  63.2 4.9 %collective-permute-start.3 = (f32[32,128]{1,0:T(8,128)S(1)}, f32[32,128]{1,0:T(8,128)S(1)}, u32[]{:S(2)}, u32[]{:S(2)}) collective-permute-start(f32[32,128]{1,0:T(8,128)S(1)} %get-tuple-element.20), channel_id=1, source_target_pairs={{1,0},{2,1},{3,2},{4,3},{5,4},{6,5},{7,6},{0,7},{9,8},{10,9},{11,1... | collective-permute-start | bytes 49160 | tf_op jit(solution)/shard_map/ppermute | solution.py:500

commit v3 on v2

--- a/solution.py
+++ b/solution.py
@@ -11,9 +11,9 @@
 
 LANES = 128
 POINTS = 20
-GROUP = 4
+GROUPS = (2, 4, 6, 5, 3)
 SLICES = 4
-AHEAD = 8
+AHEAD = 10
 BLOCKS_AHEAD = 4
 IH, LOW, INV, ROWS = 0, 20, 40, 60
 
@@ -52,13 +52,13 @@
 def transform_kernel(mesh_ref, tables_hbm, spectra_ref, comp_ref, table_ref, tables_ref, held, wide, done, arrived, left):
     length = comp_ref.shape[1]
     half = length // 2
-    groups = POINTS // GROUP
 
     def copy(c):
         return pltpu.make_async_copy(spectra_ref.at[:, c], held.at[c], arrived.at[c])
 
-    def store(g, slot):
-        return pltpu.make_async_copy(done.at[slot], comp_ref.at[pl.ds(g * (2 * GROUP), 2 * GROUP)], left.at[slot])
+    def store(start, size, slot):
+        planes = pl.ds(2 * start, 2 * size)
+        return pltpu.make_async_copy(done.at[slot, pl.ds(0, 2 * size)], comp_ref.at[planes], left.at[slot])
 
     tables_copy = pltpu.make_async_copy(tables_hbm, tables_ref, left.at[2])
     copy(0).start()
@@ -68,23 +68,17 @@
     spline_table(mesh_ref, table_ref)
     tables_copy.wait()
 
-    def group(g, carry):
-        slot = lax.rem(g, 2)
-
-        @pl.when(g >= 2)
-        def _():
-            store(g - 2, slot).wait()
-
-        for i in range(GROUP):
-            c = g * GROUP + i
+    starts = [sum(GROUPS[:g]) for g in range(len(GROUPS))]
+    for g, (start, size) in enumerate(zip(starts, GROUPS)):
+        slot = g % 2
+        if g >= 2:
+            store(starts[g - 2], GROUPS[g - 2], slot).wait()
+        for c in range(start, start + size):
             copy(c).wait()
-
-            @pl.when(c + AHEAD < POINTS)
-            def _():
+            if c + AHEAD < POINTS:
                 copy(c + AHEAD).start()
-
-        for i in range(GROUP):
-            c = g * GROUP + i
+        for i in range(size):
+            c = start + i
             for p in range(2):
                 wide[i, p] = held[c, p].astype(jnp.float32)
             parts = []
@@ -107,12 +101,9 @@
             for y in range(2):
                 done[slot, 2 * i + y, :half, :] = total[:, y * LANES : (y + 1) * LANES]
                 done[slot, 2 * i + y, half:, :] = difference[:, y * LANES : (y + 1) * LANES]
-        store(g, slot).start()
-        return carry
-
-    lax.fori_loop(0, groups, group, 0)
-    for g in range(groups - 2, groups):
-        store(g, g % 2).wait()
+        store(start, size, slot).start()
+    for g in range(len(GROUPS) - 2, len(GROUPS)):
+        store(starts[g], GROUPS[g], g % 2).wait()
 
 
 def transform(spectra, kernel_mesh):
@@ -134,8 +125,8 @@
         scratch_shapes=[
             pltpu.VMEM((2, length // 2, length), jnp.bfloat16),
             pltpu.VMEM((comps, 2, 2 * length, LANES), jnp.bfloat16),
-            pltpu.VMEM((GROUP, 2, 2 * length, LANES), jnp.float32),
-            pltpu.VMEM((2, 2 * GROUP, length, LANES), jnp.float32),
+            pltpu.VMEM((max(GROUPS), 2, 2 * length, LANES), jnp.float32),
+            pltpu.VMEM((2, 2 * max(GROUPS), length, LANES), jnp.float32),
             pltpu.SemaphoreType.DMA((comps,)),
             pltpu.SemaphoreType.DMA((3,)),
         ],
@@ -168,24 +159,35 @@
 
 
 def evaluate(comp, second, mesh, wave):
+    top = wave >= mesh(16)
+
+    def halve(nodes, past):
+        half = len(nodes) // 2
+        return [jnp.where(past, nodes[half + k], nodes[k]) for k in range(half + 1)]
+
+    def spread(node):
+        nodes = [node(k) for k in range(17)]
+        return [jnp.where(top, node(16 + k), nodes[k]) for k in range(4)] + nodes[4:]
+
+    nodes, turns = spread(mesh), []
+    for half in (8, 4, 2, 1):
+        past = wave >= nodes[half]
+        if half >= 4:
+            past = past & ~top
+        if half == 1:
+            past = past & (wave < mesh(POINTS - 2))
+        turns.append(past)
+        nodes = halve(nodes, past)
+    low, high = nodes
+
     def pick(node):
-        held = [node(POINTS - 4 + i) for i in range(4)]
-        for first in range(POINTS - 7, 0, -3):
-            below = wave < mesh(first + 3)
-            held = [jnp.where(below, node(first + i), held[i]) for i in range(4)]
-        below = wave < mesh(1)
-        return [jnp.where(below, node(min(i, 1)), held[i]) for i in range(4)]
-
-    def ends(four, past_one, past_two):
-        lower = jnp.where(past_two, four[2], jnp.where(past_one, four[1], four[0]))
-        upper = jnp.where(past_two, four[3], jnp.where(past_one, four[2], four[1]))
-        return lower, upper
-
-    points_four = pick(mesh)
-    past_one, past_two = wave >= points_four[1], wave >= points_four[2]
-    low, high = ends(points_four, past_one, past_two)
-    comp_low, comp_high = ends(pick(comp), past_one, past_two)
-    second_low, second_high = ends(pick(second), past_one, past_two)
+        nodes = spread(node)
+        for past in turns:
+            nodes = halve(nodes, past)
+        return nodes
+
+    comp_low, comp_high = pick(comp)
+    second_low, second_high = pick(second)
     width = high - low
     inverse = 1.0 / width
     a = (high - wave) * inverse
@@ -472,7 +474,7 @@
         turn_kernel,
         in_specs=[pl.BlockSpec(memory_space=pltpu.HBM)],
         out_specs=pl.BlockSpec(memory_space=pltpu.VMEM),
-        out_shape=jax.ShapeDtypeStruct((rows * width, LANES), jnp.float32),
+        out_shape=pltpu.VMEM((rows * width, LANES), jnp.float32),
         scratch_shapes=[pltpu.VMEM(wave.shape, jnp.float32), pltpu.SemaphoreType.DMA((SLICES,))],
         compiler_params=pltpu.CompilerParams(vmem_limit_bytes=8 * 1024 * 1024),
         name="turn",

time: 69.9 us -> 68.5 us (0.980)
  Pallas kernels: 30 us -> 28.7 us
  starting transfers between devices: 23.8 us -> 22.8 us
  waiting for transfers between devices: 15.4 us -> 16.4 us
    all_to_all x1, starting transfers between devices: 6.18 us -> 5.21 us  [shards(): got = lax.all_to_all(sent, 'gx', 0, 0, tiled=True).reshape(-1, LANES)]
    all_to_all x1, waiting for transfers between devices: 1.06 us -> 2.03 us  [shards(): wave = lax.all_to_all(wave, 'gx', 0, 0, tiled=True)]
    pallas_call x1, Pallas kernels: 12.7 us -> 11.7 us  [transform(): pl.pallas_call(transform_kernel, in_specs=[pl.BlockSpec(memory_space=pltp...]
  transfers between devices with their start and end apart: 6 -> 6, of which waited for: 2 -> 2; matrix products, arithmetic and copies ran while one was open for 0% -> 0% of each run, Pallas kernels for 24% -> 23%
where the time goes in v3:
time: 68.5 us; the launch traced here: 67.9 us
  Pallas kernels  28.7 us (42%)
  starting transfers between devices  22.8 us (33%)
  waiting for transfers between devices  16.4 us (24%)
    all_to_all x1, waiting for transfers between devices, shards(): got = lax.all_to_all(sent, 'gx', 0, 0, tiled=True).reshape(-1, LANES)  14.3 us
    pallas_call x1, Pallas kernels, transform(): pl.pallas_call(transform_kernel, in_specs=[pl.BlockSpec(memory_space=pltp...  11.7 us
    pallas_call x1, Pallas kernels, splines(): pl.pallas_call(functools.partial(spline_kernel, length ** (-0.5)), in_spe...  9.65 us
    all_to_all x1, starting transfers between devices, shards(): wave = lax.all_to_all(wave, 'gx', 0, 0, tiled=True)  8.01 us
    all_to_all x1, starting transfers between devices, shards(): got = lax.all_to_all(sent, 'gx', 0, 0, tiled=True).reshape(-1, LANES)  5.21 us
    ppermute x1, starting transfers between devices, shards(): lax.ppermute(push[:1], 'gx', backward)  4.95 us
    ppermute x1, starting transfers between devices, shards(): high = lax.ppermute(third_low, 'yz', backward)  2.64 us
    pallas_call x1, Pallas kernels, inner(): pl.pallas_call(inner_kernel, in_specs=[vmem, vmem, hbm, hbm, hbm], out_sp...  2.21 us
  transfers between devices with their start and end apart: 6, of which 2 were waited for; matrix products, arithmetic and copies ran while one was open for 0% of the time, Pallas kernels for 23%

profile of v3, /device:TPU:0, one launch (start us, length us, event | category | flops | bytes accessed | tf_op | source)
XLA Modules:
  0.0 67.9 jit_solution(11759194227070815887)
XLA Ops:
  0.0 0.0 copy-start
  0.0 2.1 %turn.1 = f32[1280,128]{1,0:T(8,128)} custom-call(f32[40,32,128]{2,1,0:T(8,128)} %wave_ref.1), custom_call_target="tpu_custom_call" | custom-call | tf_op jit(solution)/shard_map/turn/pallas_call | solution.py:473
  2.1 8.0 %all-to-all-start = ((f32[16,2,40,128]{3,2,1,0:T(8,128)}), f32[16,2,40,128]{3,2,1,0:T(8,128)S(1)}, u32[]{:S(2)}, u32[]{:S(2)}) async-start(f32[16,2,40,128]{3,2,1,0:T(8,128)} %bitcast.1), calls=%async_computation | async-start | bytes 1310720 | tf_op jit(solution)/shard_map/all_to_all | solution.py:488
  10.1 0.0 copy-done
  10.1 11.7 %transform.1 = (f32[40,640,128]{2,1,0:T(8,128)}, f32[60,8,128]{2,1,0:T(8,128)S(1)}) custom-call(f32[20]{0:T(128)S(1)} %copy-done, bf16[2,320,640]{2,1,0:T(8,128)(2,1)} %constant.2.clone.tables_hbm, bf16[2,20,1280,128]{3,2,1,0:T(8,128)(2,1)} %bitcast.5), custom_call_target="tpu_custom_call" | custom-call | flops 4194304000 | bytes 39321600 | tf_op jit(solution)/shard_map/transform/pallas_call | solution.py:113
  21.8 2.0 %all-to-all-done.wave_ref = f32[16,2,40,128]{3,2,1,0:T(8,128)S(1)} async-done(((f32[16,2,40,128]{3,2,1,0:T(8,128)}), f32[16,2,40,128]{3,2,1,0:T(8,128)S(1)}, u32[]{:S(2)}, u32[]{:S(2)}) %all-to-all-start) | async-done | bytes 655392 | tf_op jit(solution)/shard_map/all_to_all | solution.py:488
  23.8 9.7 %splines.1 = (f32[16,168,128]{2,1,0:T(8,128)}, f32[8,128]{1,0:T(8,128)S(1)}) custom-call(f32[20]{0:T(128)S(1)} %copy-done, f32[60,8,128]{2,1,0:T(8,128)S(1)} %get-tuple-element.13.table_ref, f32[16,2,40,128]{3,2,1,0:T(8,128)S(1)} %all-to-all-done.wave_ref, f32[40,640,128]{2,1,0:T(8,128)} %get-tuple-element.14.comp_ref), custom_call_target="tpu_custom_call" | custom-call | tf_op jit(solution)/shard_map/splines/pallas_call | solution.py:275
  33.5 5.2 %all-to-all-start.1 = ((f32[16,168,128]{2,1,0:T(8,128)}), f32[16,168,128]{2,1,0:T(8,128)S(1)}, u32[]{:S(2)}, u32[]{:S(2)}) async-start(f32[16,168,128]{2,1,0:T(8,128)} %get-tuple-element.15), calls=%async_computation.1 | async-start | bytes 2752512 | tf_op jit(solution)/shard_map/all_to_all | solution.py:491
  38.7 1.9 %edges.1 = (f32[2,32,128]{2,1,0:T(8,128)S(1)}, f32[2,32,128]{2,1,0:T(8,128)S(1)}) custom-call(f32[8,128]{1,0:T(8,128)S(1)} %get-tuple-element.16.order_ref, f32[40,32,128]{2,1,0:T(8,128)} %density_ref.3, f32[3,40,32,128]{3,2,1,0:T(8,128)} %gradient_ref.3), custom_call_target="tpu_custom_call" | custom-call | tf_op jit(solution)/shard_map/edges/pallas_call | solution.py:320
  40.6 0.5 collective-permute-start
  41.1 5.0 %collective-permute-start.1 = (f32[1,32,128]{2,1,0:T(8,128)S(1)}, f32[1,32,128]{2,1,0:T(8,128)S(1)}, u32[]{:S(2)}, u32[]{:S(2)}) collective-permute-start(f32[1,32,128]{2,1,0:T(8,128)S(1)} %get-tuple-element.22), channel_id=1, source_target_pairs={{8,0},{16,8},{24,16},{32,24},{40,32},{48,40},{56,48},{64,56},{72,6... | collective-permute-start | bytes 49160 | tf_op jit(solution)/shard_map/ppermute | solution.py:496
  46.0 14.3 %all-to-all-done.1 = f32[16,168,128]{2,1,0:T(8,128)S(1)} async-done(((f32[16,168,128]{2,1,0:T(8,128)}), f32[16,168,128]{2,1,0:T(8,128)S(1)}, u32[]{:S(2)}, u32[]{:S(2)}) %all-to-all-start.1) | async-done | bytes 1376288 | tf_op jit(solution)/shard_map/all_to_all | solution.py:491
  60.3 1.5 %collective-permute-start.2 = (f32[32,128]{1,0:T(8,128)S(1)}, f32[32,128]{1,0:T(8,128)S(1)}, u32[]{:S(2)}, u32[]{:S(2)}) collective-permute-start(f32[32,128]{1,0:T(8,128)S(1)} %get-tuple-element.19), channel_id=1, source_target_pairs={{0,1},{1,2},{2,3},{3,4},{4,5},{5,6},{6,7},{7,0},{8,9},{9,10},{10,1... | collective-permute-start | bytes 49160 | tf_op jit(solution)/shard_map/ppermute | solution.py:501
  61.8 2.6 %collective-permute-start.3 = (f32[32,128]{1,0:T(8,128)S(1)}, f32[32,128]{1,0:T(8,128)S(1)}, u32[]{:S(2)}, u32[]{:S(2)}) collective-permute-start(f32[32,128]{1,0:T(8,128)S(1)} %get-tuple-element.20), channel_id=1, source_target_pairs={{1,0},{2,1},{3,2},{4,3},{5,4},{6,5},{7,6},{0,7},{9,8},{10,9},{11,1... | collective-permute-start | bytes 49160 | tf_op jit(solution)/shard_map/ppermute | solution.py:502
  64.5 0.0 collective-permute-done
  64.5 0.0 collective-permute-done.1
  64.5 2.2 %inner.1.part_ref = f32[40,32,128]{2,1,0:T(8,128)S(1)} custom-call(f32[2688,128]{1,0:T(8,128)S(1)} %bitcast.4, f32[2,32,128]{2,1,0:T(8,128)S(1)} %pad_maximum_fusion.push_ref, f32[40,32,128]{2,1,0:T(8,128)} %density_ref.3, f32[40,32,128]{2,1,0:T(8,128)} %rate_ref.1, f32[3,40,32,128]{3,2,1,0:T(8,128)} %gradient_ref.3), custom_call_target="tpu_custom_call" | custom-call | tf_op jit(solution)/shard_map/inner/pallas_call | solution.py:401
  66.7 0.0 collective-permute-done.2.low_ref
  66.7 0.0 collective-permute-done.3.high_ref
  66.7 1.2 %outer.1 = f32[40,32,128]{2,1,0:T(8,128)} custom-call(f32[40,32,128]{2,1,0:T(8,128)S(1)} %inner.1.part_ref, f32[32,128]{1,0:T(8,128)S(1)} %collective-permute-done.2.low_ref, f32[32,128]{1,0:T(8,128)S(1)} %collective-permute-done.3.high_ref), custom_call_target="tpu_custom_call" | custom-call | tf_op jit(solution)/shard_map/outer/pallas_call | solution.py:438
  (3 shorter events, 0.0 us)
Async XLA Ops:
  0.0 10.1 %copy-start = (f32[20]{0:T(128)S(1)}, f32[20]{0:T(128)}, u32[]{:S(2)}) copy-start(f32[20]{0:T(128)} %mesh_ref.3) | copy-start | bytes 244
  2.1 21.8 %all-to-all-start = ((f32[16,2,40,128]{3,2,1,0:T(8,128)}), f32[16,2,40,128]{3,2,1,0:T(8,128)S(1)}, u32[]{:S(2)}, u32[]{:S(2)}) async-start(f32[16,2,40,128]{3,2,1,0:T(8,128)} %bitcast.1), calls=%async_computation | async-start | bytes 1310720 | tf_op jit(solution)/shard_map/all_to_all | solution.py:488
  33.5 26.9 %all-to-all-start.1 = ((f32[16,168,128]{2,1,0:T(8,128)}), f32[16,168,128]{2,1,0:T(8,128)S(1)}, u32[]{:S(2)}, u32[]{:S(2)}) async-start(f32[16,168,128]{2,1,0:T(8,128)} %get-tuple-element.15), calls=%async_computation.1 | async-start | bytes 2752512 | tf_op jit(solution)/shard_map/all_to_all | solution.py:491
  40.6 23.9 %collective-permute-start = (f32[1,32,128]{2,1,0:T(8,128)S(1)}, f32[1,32,128]{2,1,0:T(8,128)S(1)}, u32[]{:S(2)}, u32[]{:S(2)}) collective-permute-start(f32[1,32,128]{2,1,0:T(8,128)S(1)} %get-tuple-element.21), channel_id=1, source_target_pairs={{0,8},{8,16},{16,24},{24,32},{32,40},{40,48},{48,56},{56,64},{64,7... | collective-permute-start | bytes 49160 | tf_op jit(solution)/shard_map/ppermute | solution.py:496
  41.1 23.4 %collective-permute-start.1 = (f32[1,32,128]{2,1,0:T(8,128)S(1)}, f32[1,32,128]{2,1,0:T(8,128)S(1)}, u32[]{:S(2)}, u32[]{:S(2)}) collective-permute-start(f32[1,32,128]{2,1,0:T(8,128)S(1)} %get-tuple-element.22), channel_id=1, source_target_pairs={{8,0},{16,8},{24,16},{32,24},{40,32},{48,40},{56,48},{64,56},{72,6... | collective-permute-start | bytes 49160 | tf_op jit(solution)/shard_map/ppermute | solution.py:496
  60.3 6.4 %collective-permute-start.2 = (f32[32,128]{1,0:T(8,128)S(1)}, f32[32,128]{1,0:T(8,128)S(1)}, u32[]{:S(2)}, u32[]{:S(2)}) collective-permute-start(f32[32,128]{1,0:T(8,128)S(1)} %get-tuple-element.19), channel_id=1, source_target_pairs={{0,1},{1,2},{2,3},{3,4},{4,5},{5,6},{6,7},{7,0},{8,9},{9,10},{10,1... | collective-permute-start | bytes 49160 | tf_op jit(solution)/shard_map/ppermute | solution.py:501
  61.8 4.9 %collective-permute-start.3 = (f32[32,128]{1,0:T(8,128)S(1)}, f32[32,128]{1,0:T(8,128)S(1)}, u32[]{:S(2)}, u32[]{:S(2)}) collective-permute-start(f32[32,128]{1,0:T(8,128)S(1)} %get-tuple-element.20), channel_id=1, source_target_pairs={{1,0},{2,1},{3,2},{4,3},{5,4},{6,5},{7,6},{0,7},{9,8},{10,9},{11,1... | collective-permute-start | bytes 49160 | tf_op jit(solution)/shard_map/ppermute | solution.py:502

commit v4 on v3

--- a/solution.py
+++ b/solution.py
@@ -11,7 +11,8 @@
 
 LANES = 128
 POINTS = 20
-GROUPS = (2, 4, 6, 5, 3)
+KEPT = 4
+GROUPS = (2, 4, 6, 4, 4)
 SLICES = 4
 AHEAD = 10
 BLOCKS_AHEAD = 4
@@ -49,7 +50,7 @@
     table_ref[LOW + POINTS - 1] = low
 
 
-def transform_kernel(mesh_ref, tables_hbm, spectra_ref, comp_ref, table_ref, tables_ref, held, wide, done, arrived, left):
+def transform_kernel(mesh_ref, tables_hbm, spectra_ref, comp_ref, kept_ref, table_ref, tables_ref, held, wide, done, arrived, left):
     length = comp_ref.shape[1]
     half = length // 2
 
@@ -57,6 +58,7 @@
         return pltpu.make_async_copy(spectra_ref.at[:, c], held.at[c], arrived.at[c])
 
     def store(start, size, slot):
+        size = min(size, POINTS - KEPT - start)
         planes = pl.ds(2 * start, 2 * size)
         return pltpu.make_async_copy(done.at[slot, pl.ds(0, 2 * size)], comp_ref.at[planes], left.at[slot])
 
@@ -69,9 +71,10 @@
     tables_copy.wait()
 
     starts = [sum(GROUPS[:g]) for g in range(len(GROUPS))]
+    sent = [g for g in range(len(GROUPS)) if starts[g] < POINTS - KEPT]
     for g, (start, size) in enumerate(zip(starts, GROUPS)):
         slot = g % 2
-        if g >= 2:
+        if g >= 2 and g in sent:
             store(starts[g - 2], GROUPS[g - 2], slot).wait()
         for c in range(start, start + size):
             copy(c).wait()
@@ -99,10 +102,15 @@
                 parts.append(jnp.dot(tables_ref[parity], operand, preferred_element_type=jnp.float32))
             total, difference = parts[0] + parts[1], parts[0] - parts[1]
             for y in range(2):
-                done[slot, 2 * i + y, :half, :] = total[:, y * LANES : (y + 1) * LANES]
-                done[slot, 2 * i + y, half:, :] = difference[:, y * LANES : (y + 1) * LANES]
-        store(start, size, slot).start()
-    for g in range(len(GROUPS) - 2, len(GROUPS)):
+                if c < POINTS - KEPT:
+                    plane = done.at[slot, 2 * i + y]
+                else:
+                    plane = kept_ref.at[2 * (c - POINTS + KEPT) + y]
+                plane[:half, :] = total[:, y * LANES : (y + 1) * LANES]
+                plane[half:, :] = difference[:, y * LANES : (y + 1) * LANES]
+        if g in sent:
+            store(start, size, slot).start()
+    for g in sent[-2:]:
         store(starts[g], GROUPS[g], g % 2).wait()
 
 
@@ -117,9 +125,10 @@
             pl.BlockSpec(memory_space=pltpu.HBM),
             pl.BlockSpec(memory_space=pltpu.HBM),
         ],
-        out_specs=[pl.BlockSpec(memory_space=pltpu.HBM), pl.BlockSpec(memory_space=pltpu.VMEM)],
+        out_specs=[pl.BlockSpec(memory_space=pltpu.HBM)] + [pl.BlockSpec(memory_space=pltpu.VMEM)] * 2,
         out_shape=[
-            pltpu.HBM((2 * comps, length, LANES), jnp.float32),
+            pltpu.HBM((2 * (comps - KEPT), length, LANES), jnp.float32),
+            jax.ShapeDtypeStruct((2 * KEPT, length, LANES), jnp.float32),
             jax.ShapeDtypeStruct((ROWS, 8, LANES), jnp.float32),
         ],
         scratch_shapes=[
@@ -203,7 +212,7 @@
     return value, slope
 
 
-def spline_kernel(scale, mesh_ref, table_ref, wave_ref, comp_ref, out_hbm, order_ref, out_ref, held, arrived, left):
+def spline_kernel(scale, mesh_ref, table_ref, wave_ref, kept_ref, comp_ref, out_hbm, order_ref, out_ref, held, arrived, left):
     count, width = wave_ref.shape[0], wave_ref.shape[2]
     tiles = width // 8
     part = 2 * width + 4
@@ -242,7 +251,13 @@
         turn(previous)
         for y in range(2):
             wave = wave_ref[block, y].reshape(tiles, 8, LANES)
-            comp = lambda j: held[block, 2 * j + y].reshape(tiles, 8, LANES)
+
+            def comp(j):
+                if j < POINTS - KEPT:
+                    return held[block, 2 * j + y].reshape(tiles, 8, LANES)
+                rows = pl.ds(pl.multiple_of(block * width, 8), width)
+                return kept_ref[2 * (j - POINTS + KEPT) + y, rows, :].reshape(tiles, 8, LANES)
+
             second = solve(comp, lambda j: table_ref[j])
             value, slope = evaluate(comp, lambda j: second[j], lambda j: mesh[j], wave)
             value = (value * scale).reshape(width, LANES)
@@ -266,7 +281,7 @@
         store(block).wait()
 
 
-def splines(kernel_mesh, comp, table, wave):
+def splines(kernel_mesh, comp, kept, table, wave):
     count, width = wave.shape[0], wave.shape[2]
     planes, length = comp.shape[0], comp.shape[1]
     vmem = pl.BlockSpec(memory_space=pltpu.VMEM)
@@ -274,7 +289,7 @@
     message = (count, 4 * width + 8, LANES)
     return pl.pallas_call(
         functools.partial(spline_kernel, length ** (-0.5)),
-        in_specs=[pl.BlockSpec(memory_space=pltpu.SMEM), vmem, vmem, hbm],
+        in_specs=[pl.BlockSpec(memory_space=pltpu.SMEM), vmem, vmem, vmem, hbm],
         out_specs=[hbm, vmem],
         out_shape=[pltpu.HBM(message, jnp.float32), jax.ShapeDtypeStruct((8, LANES), jnp.float32)],
         scratch_shapes=[
@@ -285,7 +300,7 @@
         ],
         compiler_params=pltpu.CompilerParams(vmem_limit_bytes=28 * 1024 * 1024),
         name="splines",
-    )(kernel_mesh, table, wave, in_hbm(comp))
+    )(kernel_mesh, table, wave, kept, in_hbm(comp))
 
 
 def edges_kernel(order_ref, density_ref, gradient_ref, push_ref, weight_ref, density, first, third, arrived):
@@ -486,8 +501,8 @@
     count = lax.axis_size("gx")
     wave = turn(local_wave).reshape(count, 2, width, LANES)
     wave = lax.all_to_all(wave, "gx", 0, 0, tiled=True)
-    comp, table = transform(spectra, kernel_mesh)
-    sent, order = splines(kernel_mesh, comp, table, wave)
+    comp, kept, table = transform(spectra, kernel_mesh)
+    sent, order = splines(kernel_mesh, comp, kept, table, wave)
     got = lax.all_to_all(sent, "gx", 0, 0, tiled=True).reshape(-1, LANES)
 
     push, weight = edges(order, density, wave_gradient)

time: 68.5 us -> 66.9 us (0.977)
  Pallas kernels: 28.7 us -> 27.1 us
  starting transfers between devices: 22.8 us -> 21.4 us
  waiting for transfers between devices: 16.4 us -> 17.8 us
    all_to_all x1, waiting for transfers between devices: 2.03 us -> 3.43 us  [shards(): wave = lax.all_to_all(wave, 'gx', 0, 0, tiled=True)]
    pallas_call x1, Pallas kernels: 11.7 us -> 10.3 us  [transform(): pl.pallas_call(transform_kernel, in_specs=[pl.BlockSpec(memory_space=pltp...]
    all_to_all x1, starting transfers between devices: 5.21 us -> 3.81 us  [shards(): got = lax.all_to_all(sent, 'gx', 0, 0, tiled=True).reshape(-1, LANES)]
  transfers between devices with their start and end apart: 6 -> 6, of which waited for: 2 -> 2; matrix products, arithmetic and copies ran while one was open for 0% -> 0% of each run, Pallas kernels for 23% -> 22%
where the time goes in v4:
time: 66.9 us; the launch traced here: 66.3 us
  Pallas kernels  27.1 us (41%)
  starting transfers between devices  21.4 us (32%)
  waiting for transfers between devices  17.8 us (27%)
    all_to_all x1, waiting for transfers between devices, shards(): got = lax.all_to_all(sent, 'gx', 0, 0, tiled=True).reshape(-1, LANES)  14.3 us
    pallas_call x1, Pallas kernels, transform(): pl.pallas_call(transform_kernel, in_specs=[pl.BlockSpec(memory_space=pltp...  10.3 us
    pallas_call x1, Pallas kernels, splines(): pl.pallas_call(functools.partial(spline_kernel, length ** (-0.5)), in_spe...  9.45 us
    all_to_all x1, starting transfers between devices, shards(): wave = lax.all_to_all(wave, 'gx', 0, 0, tiled=True)  8.01 us
    ppermute x1, starting transfers between devices, shards(): lax.ppermute(push[:1], 'gx', backward)  4.95 us
    all_to_all x1, starting transfers between devices, shards(): got = lax.all_to_all(sent, 'gx', 0, 0, tiled=True).reshape(-1, LANES)  3.81 us
    all_to_all x1, waiting for transfers between devices, shards(): wave = lax.all_to_all(wave, 'gx', 0, 0, tiled=True)  3.43 us
    ppermute x1, starting transfers between devices, shards(): high = lax.ppermute(third_low, 'yz', backward)  2.65 us
  transfers between devices with their start and end apart: 6, of which 2 were waited for; matrix products, arithmetic and copies ran while one was open for 0% of the time, Pallas kernels for 22%

profile of v4, /device:TPU:0, one launch (start us, length us, event | category | flops | bytes accessed | tf_op | source)
XLA Modules:
  0.0 66.3 jit_solution(12021187419467993050)
XLA Ops:
  0.0 0.0 copy-start
  0.0 2.1 %turn.1 = f32[1280,128]{1,0:T(8,128)} custom-call(f32[40,32,128]{2,1,0:T(8,128)} %wave_ref.1), custom_call_target="tpu_custom_call" | custom-call | tf_op jit(solution)/shard_map/turn/pallas_call | solution.py:488
  2.1 8.0 %all-to-all-start = ((f32[16,2,40,128]{3,2,1,0:T(8,128)}), f32[16,2,40,128]{3,2,1,0:T(8,128)S(1)}, u32[]{:S(2)}, u32[]{:S(2)}) async-start(f32[16,2,40,128]{3,2,1,0:T(8,128)} %bitcast.1), calls=%async_computation | async-start | bytes 1310720 | tf_op jit(solution)/shard_map/all_to_all | solution.py:503
  10.1 0.0 copy-done
  10.1 10.3 %transform.1 = (f32[32,640,128]{2,1,0:T(8,128)}, f32[8,640,128]{2,1,0:T(8,128)S(1)}, f32[60,8,128]{2,1,0:T(8,128)S(1)}) custom-call(f32[20]{0:T(128)S(1)} %copy-done, bf16[2,320,640]{2,1,0:T(8,128)(2,1)} %constant.2.clone.tables_hbm, bf16[2,20,1280,128]{3,2,1,0:T(8,128)(2,1)} %bitcast.5), custom_call_target="tpu_custom_call" | custom-call | flops 4194304000 | bytes 39321600 | tf_op jit(solution)/shard_map/transform/pallas_call | solution.py:121
  20.4 3.4 %all-to-all-done.wave_ref = f32[16,2,40,128]{3,2,1,0:T(8,128)S(1)} async-done(((f32[16,2,40,128]{3,2,1,0:T(8,128)}), f32[16,2,40,128]{3,2,1,0:T(8,128)S(1)}, u32[]{:S(2)}, u32[]{:S(2)}) %all-to-all-start) | async-done | bytes 655392 | tf_op jit(solution)/shard_map/all_to_all | solution.py:503
  23.8 9.5 %splines.1 = (f32[16,168,128]{2,1,0:T(8,128)}, f32[8,128]{1,0:T(8,128)S(1)}) custom-call(f32[20]{0:T(128)S(1)} %copy-done, f32[60,8,128]{2,1,0:T(8,128)S(1)} %get-tuple-element.14.table_ref, f32[16,2,40,128]{3,2,1,0:T(8,128)S(1)} %all-to-all-done.wave_ref, f32[8,640,128]{2,1,0:T(8,128)S(1)} %get-tuple-element.15.kept_ref, ...), custom_call_target="tpu_custom_call" | custom-call | tf_op jit(solution)/shard_map/splines/pallas_call | solution.py:290
  33.3 3.8 %all-to-all-start.1 = ((f32[16,168,128]{2,1,0:T(8,128)}), f32[16,168,128]{2,1,0:T(8,128)S(1)}, u32[]{:S(2)}, u32[]{:S(2)}) async-start(f32[16,168,128]{2,1,0:T(8,128)} %get-tuple-element.17), calls=%async_computation.1 | async-start | bytes 2752512 | tf_op jit(solution)/shard_map/all_to_all | solution.py:506
  37.1 1.9 %edges.1 = (f32[2,32,128]{2,1,0:T(8,128)S(1)}, f32[2,32,128]{2,1,0:T(8,128)S(1)}) custom-call(f32[8,128]{1,0:T(8,128)S(1)} %get-tuple-element.18.order_ref, f32[40,32,128]{2,1,0:T(8,128)} %density_ref.3, f32[3,40,32,128]{3,2,1,0:T(8,128)} %gradient_ref.3), custom_call_target="tpu_custom_call" | custom-call | tf_op jit(solution)/shard_map/edges/pallas_call | solution.py:335
  39.0 0.5 collective-permute-start
  39.5 5.0 %collective-permute-start.1 = (f32[1,32,128]{2,1,0:T(8,128)S(1)}, f32[1,32,128]{2,1,0:T(8,128)S(1)}, u32[]{:S(2)}, u32[]{:S(2)}) collective-permute-start(f32[1,32,128]{2,1,0:T(8,128)S(1)} %get-tuple-element.24), channel_id=1, source_target_pairs={{8,0},{16,8},{24,16},{32,24},{40,32},{48,40},{56,48},{64,56},{72,6... | collective-permute-start | bytes 49160 | tf_op jit(solution)/shard_map/ppermute | solution.py:511
  44.4 14.3 %all-to-all-done.1 = f32[16,168,128]{2,1,0:T(8,128)S(1)} async-done(((f32[16,168,128]{2,1,0:T(8,128)}), f32[16,168,128]{2,1,0:T(8,128)S(1)}, u32[]{:S(2)}, u32[]{:S(2)}) %all-to-all-start.1) | async-done | bytes 1376288 | tf_op jit(solution)/shard_map/all_to_all | solution.py:506
  58.7 1.5 %collective-permute-start.2 = (f32[32,128]{1,0:T(8,128)S(1)}, f32[32,128]{1,0:T(8,128)S(1)}, u32[]{:S(2)}, u32[]{:S(2)}) collective-permute-start(f32[32,128]{1,0:T(8,128)S(1)} %get-tuple-element.21), channel_id=1, source_target_pairs={{0,1},{1,2},{2,3},{3,4},{4,5},{5,6},{6,7},{7,0},{8,9},{9,10},{10,1... | collective-permute-start | bytes 49160 | tf_op jit(solution)/shard_map/ppermute | solution.py:516
  60.2 2.6 %collective-permute-start.3 = (f32[32,128]{1,0:T(8,128)S(1)}, f32[32,128]{1,0:T(8,128)S(1)}, u32[]{:S(2)}, u32[]{:S(2)}) collective-permute-start(f32[32,128]{1,0:T(8,128)S(1)} %get-tuple-element.22), channel_id=1, source_target_pairs={{1,0},{2,1},{3,2},{4,3},{5,4},{6,5},{7,6},{0,7},{9,8},{10,9},{11,1... | collective-permute-start | bytes 49160 | tf_op jit(solution)/shard_map/ppermute | solution.py:517
  62.9 0.0 collective-permute-done
  62.9 0.0 collective-permute-done.1
  62.9 2.2 %inner.1.part_ref = f32[40,32,128]{2,1,0:T(8,128)S(1)} custom-call(f32[2688,128]{1,0:T(8,128)S(1)} %bitcast.4, f32[2,32,128]{2,1,0:T(8,128)S(1)} %pad_maximum_fusion.push_ref, f32[40,32,128]{2,1,0:T(8,128)} %density_ref.3, f32[40,32,128]{2,1,0:T(8,128)} %rate_ref.1, f32[3,40,32,128]{3,2,1,0:T(8,128)} %gradient_ref.3), custom_call_target="tpu_custom_call" | custom-call | tf_op jit(solution)/shard_map/inner/pallas_call | solution.py:416
  65.1 0.0 collective-permute-done.2.low_ref
  65.1 0.0 collective-permute-done.3.high_ref
  65.1 1.2 %outer.1 = f32[40,32,128]{2,1,0:T(8,128)} custom-call(f32[40,32,128]{2,1,0:T(8,128)S(1)} %inner.1.part_ref, f32[32,128]{1,0:T(8,128)S(1)} %collective-permute-done.2.low_ref, f32[32,128]{1,0:T(8,128)S(1)} %collective-permute-done.3.high_ref), custom_call_target="tpu_custom_call" | custom-call | tf_op jit(solution)/shard_map/outer/pallas_call | solution.py:453
  (3 shorter events, 0.0 us)
Async XLA Ops:
  0.0 10.1 %copy-start = (f32[20]{0:T(128)S(1)}, f32[20]{0:T(128)}, u32[]{:S(2)}) copy-start(f32[20]{0:T(128)} %mesh_ref.3) | copy-start | bytes 244
  2.1 21.8 %all-to-all-start = ((f32[16,2,40,128]{3,2,1,0:T(8,128)}), f32[16,2,40,128]{3,2,1,0:T(8,128)S(1)}, u32[]{:S(2)}, u32[]{:S(2)}) async-start(f32[16,2,40,128]{3,2,1,0:T(8,128)} %bitcast.1), calls=%async_computation | async-start | bytes 1310720 | tf_op jit(solution)/shard_map/all_to_all | solution.py:503
  33.3 25.5 %all-to-all-start.1 = ((f32[16,168,128]{2,1,0:T(8,128)}), f32[16,168,128]{2,1,0:T(8,128)S(1)}, u32[]{:S(2)}, u32[]{:S(2)}) async-start(f32[16,168,128]{2,1,0:T(8,128)} %get-tuple-element.17), calls=%async_computation.1 | async-start | bytes 2752512 | tf_op jit(solution)/shard_map/all_to_all | solution.py:506
  39.0 23.9 %collective-permute-start = (f32[1,32,128]{2,1,0:T(8,128)S(1)}, f32[1,32,128]{2,1,0:T(8,128)S(1)}, u32[]{:S(2)}, u32[]{:S(2)}) collective-permute-start(f32[1,32,128]{2,1,0:T(8,128)S(1)} %get-tuple-element.23), channel_id=1, source_target_pairs={{0,8},{8,16},{16,24},{24,32},{32,40},{40,48},{48,56},{56,64},{64,7... | collective-permute-start | bytes 49160 | tf_op jit(solution)/shard_map/ppermute | solution.py:511
  39.5 23.4 %collective-permute-start.1 = (f32[1,32,128]{2,1,0:T(8,128)S(1)}, f32[1,32,128]{2,1,0:T(8,128)S(1)}, u32[]{:S(2)}, u32[]{:S(2)}) collective-permute-start(f32[1,32,128]{2,1,0:T(8,128)S(1)} %get-tuple-element.24), channel_id=1, source_target_pairs={{8,0},{16,8},{24,16},{32,24},{40,32},{48,40},{56,48},{64,56},{72,6... | collective-permute-start | bytes 49160 | tf_op jit(solution)/shard_map/ppermute | solution.py:511
  58.7 6.4 %collective-permute-start.2 = (f32[32,128]{1,0:T(8,128)S(1)}, f32[32,128]{1,0:T(8,128)S(1)}, u32[]{:S(2)}, u32[]{:S(2)}) collective-permute-start(f32[32,128]{1,0:T(8,128)S(1)} %get-tuple-element.21), channel_id=1, source_target_pairs={{0,1},{1,2},{2,3},{3,4},{4,5},{5,6},{6,7},{7,0},{8,9},{9,10},{10,1... | collective-permute-start | bytes 49160 | tf_op jit(solution)/shard_map/ppermute | solution.py:516
  60.2 4.9 %collective-permute-start.3 = (f32[32,128]{1,0:T(8,128)S(1)}, f32[32,128]{1,0:T(8,128)S(1)}, u32[]{:S(2)}, u32[]{:S(2)}) collective-permute-start(f32[32,128]{1,0:T(8,128)S(1)} %get-tuple-element.22), channel_id=1, source_target_pairs={{1,0},{2,1},{3,2},{4,3},{5,4},{6,5},{7,6},{0,7},{9,8},{10,9},{11,1... | collective-permute-start | bytes 49160 | tf_op jit(solution)/shard_map/ppermute | solution.py:517

commit v5 on v4

--- a/solution.py
+++ b/solution.py
@@ -415,7 +415,7 @@
     vmem, hbm = pl.BlockSpec(memory_space=pltpu.VMEM), pl.BlockSpec(memory_space=pltpu.HBM)
     return pl.pallas_call(
         inner_kernel,
-        in_specs=[vmem, vmem, hbm, hbm, hbm],
+        in_specs=[vmem, vmem, pl.BlockSpec(memory_space=pl.ANY), pl.BlockSpec(memory_space=pl.ANY), hbm],
         out_specs=vmem,
         out_shape=jax.ShapeDtypeStruct(density.shape, jnp.float32),
         scratch_shapes=[
@@ -426,7 +426,7 @@
         ],
         compiler_params=pltpu.CompilerParams(vmem_limit_bytes=16 * 1024 * 1024),
         name="inner",
-    )(got, push, in_hbm(density), in_hbm(rate), in_hbm(gradient))
+    )(got, push, density, rate, in_hbm(gradient))
 
 
 def outer_kernel(part_ref, low_ref, high_ref, out_hbm, out_ref, left):

time: 66.9 us -> 67.6 us (1.010)
  Pallas kernels: 27.1 us -> 28 us
    pallas_call x1, Pallas kernels: 2.21 us -> 3.07 us  [inner(): pl.pallas_call(inner_kernel, in_specs=[vmem, vmem, pl.BlockSpec(memory_sp...]
  transfers between devices with their start and end apart: 6 -> 6, of which waited for: 2 -> 2; matrix products, arithmetic and copies ran while one was open for 0% -> 0% of each run, Pallas kernels for 22% -> 23%
where the time goes in v5:
time: 67.6 us; the launch traced here: 67.2 us
  Pallas kernels  28 us (41%)
  starting transfers between devices  21.4 us (32%)
  waiting for transfers between devices  17.6 us (26%)
    all_to_all x1, waiting for transfers between devices, shards(): got = lax.all_to_all(sent, 'gx', 0, 0, tiled=True).reshape(-1, LANES)  14.2 us
    pallas_call x1, Pallas kernels, transform(): pl.pallas_call(transform_kernel, in_specs=[pl.BlockSpec(memory_space=pltp...  10.3 us
    pallas_call x1, Pallas kernels, splines(): pl.pallas_call(functools.partial(spline_kernel, length ** (-0.5)), in_spe...  9.46 us
    all_to_all x1, starting transfers between devices, shards(): wave = lax.all_to_all(wave, 'gx', 0, 0, tiled=True)  8.01 us
    ppermute x1, starting transfers between devices, shards(): lax.ppermute(push[:1], 'gx', backward)  4.95 us
    all_to_all x1, starting transfers between devices, shards(): got = lax.all_to_all(sent, 'gx', 0, 0, tiled=True).reshape(-1, LANES)  3.82 us
    all_to_all x1, waiting for transfers between devices, shards(): wave = lax.all_to_all(wave, 'gx', 0, 0, tiled=True)  3.42 us
    pallas_call x1, Pallas kernels, inner(): pl.pallas_call(inner_kernel, in_specs=[vmem, vmem, pl.BlockSpec(memory_sp...  3.07 us
  transfers between devices with their start and end apart: 6, of which 2 were waited for; matrix products, arithmetic and copies ran while one was open for 0% of the time, Pallas kernels for 23%

profile of v5, /device:TPU:0, one launch (start us, length us, event | category | flops | bytes accessed | tf_op | source)
XLA Modules:
  0.0 67.2 jit_solution(16245927170771720607)
XLA Ops:
  0.0 0.0 copy-start.2
  0.0 2.1 %turn.1 = f32[1280,128]{1,0:T(8,128)} custom-call(f32[40,32,128]{2,1,0:T(8,128)} %wave_ref.1), custom_call_target="tpu_custom_call" | custom-call | tf_op jit(solution)/shard_map/turn/pallas_call | solution.py:488
  2.1 8.0 %all-to-all-start = ((f32[16,2,40,128]{3,2,1,0:T(8,128)}), f32[16,2,40,128]{3,2,1,0:T(8,128)S(1)}, u32[]{:S(2)}, u32[]{:S(2)}) async-start(f32[16,2,40,128]{3,2,1,0:T(8,128)} %bitcast.1), calls=%async_computation | async-start | bytes 1310720 | tf_op jit(solution)/shard_map/all_to_all | solution.py:503
  10.1 0.0 copy-done.2
  10.1 10.3 %transform.1 = (f32[32,640,128]{2,1,0:T(8,128)}, f32[8,640,128]{2,1,0:T(8,128)S(1)}, f32[60,8,128]{2,1,0:T(8,128)S(1)}) custom-call(f32[20]{0:T(128)S(1)} %copy-done.2, bf16[2,320,640]{2,1,0:T(8,128)(2,1)} %constant.2.clone.tables_hbm, bf16[2,20,1280,128]{3,2,1,0:T(8,128)(2,1)} %bitcast.5), custom_call_target="tpu_custom_call" | custom-call | flops 4194304000 | bytes 39321600 | tf_op jit(solution)/shard_map/transform/pallas_call | solution.py:121
  20.4 3.4 %all-to-all-done.wave_ref = f32[16,2,40,128]{3,2,1,0:T(8,128)S(1)} async-done(((f32[16,2,40,128]{3,2,1,0:T(8,128)}), f32[16,2,40,128]{3,2,1,0:T(8,128)S(1)}, u32[]{:S(2)}, u32[]{:S(2)}) %all-to-all-start) | async-done | bytes 655392 | tf_op jit(solution)/shard_map/all_to_all | solution.py:503
  23.8 9.5 %splines.1 = (f32[16,168,128]{2,1,0:T(8,128)}, f32[8,128]{1,0:T(8,128)S(1)}) custom-call(f32[20]{0:T(128)S(1)} %copy-done.2, f32[60,8,128]{2,1,0:T(8,128)S(1)} %get-tuple-element.14.table_ref, f32[16,2,40,128]{3,2,1,0:T(8,128)S(1)} %all-to-all-done.wave_ref, f32[8,640,128]{2,1,0:T(8,128)S(1)} %get-tuple-element.15.kept_ref, ...), custom_call_target="tpu_custom_call" | custom-call | tf_op jit(solution)/shard_map/splines/pallas_call | solution.py:290
  33.3 3.8 %all-to-all-start.1 = ((f32[16,168,128]{2,1,0:T(8,128)}), f32[16,168,128]{2,1,0:T(8,128)S(1)}, u32[]{:S(2)}, u32[]{:S(2)}) async-start(f32[16,168,128]{2,1,0:T(8,128)} %get-tuple-element.17), calls=%async_computation.1 | async-start | bytes 2752512 | tf_op jit(solution)/shard_map/all_to_all | solution.py:506
  37.1 0.0 copy-start
  37.1 0.0 copy-start.1
  37.1 2.0 %edges.1 = (f32[2,32,128]{2,1,0:T(8,128)S(1)}, f32[2,32,128]{2,1,0:T(8,128)S(1)}) custom-call(f32[8,128]{1,0:T(8,128)S(1)} %get-tuple-element.18.order_ref, f32[40,32,128]{2,1,0:T(8,128)} %density_ref.3, f32[3,40,32,128]{3,2,1,0:T(8,128)} %gradient_ref.3), custom_call_target="tpu_custom_call" | custom-call | tf_op jit(solution)/shard_map/edges/pallas_call | solution.py:335
  39.1 0.5 collective-permute-start
  39.6 5.0 %collective-permute-start.1 = (f32[1,32,128]{2,1,0:T(8,128)S(1)}, f32[1,32,128]{2,1,0:T(8,128)S(1)}, u32[]{:S(2)}, u32[]{:S(2)}) collective-permute-start(f32[1,32,128]{2,1,0:T(8,128)S(1)} %get-tuple-element.24), channel_id=1, source_target_pairs={{8,0},{16,8},{24,16},{32,24},{40,32},{48,40},{56,48},{64,56},{72,6... | collective-permute-start | bytes 49160 | tf_op jit(solution)/shard_map/ppermute | solution.py:511
  44.6 14.2 %all-to-all-done.1 = f32[16,168,128]{2,1,0:T(8,128)S(1)} async-done(((f32[16,168,128]{2,1,0:T(8,128)}), f32[16,168,128]{2,1,0:T(8,128)S(1)}, u32[]{:S(2)}, u32[]{:S(2)}) %all-to-all-start.1) | async-done | bytes 1376288 | tf_op jit(solution)/shard_map/all_to_all | solution.py:506
  58.8 1.5 %collective-permute-start.2 = (f32[32,128]{1,0:T(8,128)S(1)}, f32[32,128]{1,0:T(8,128)S(1)}, u32[]{:S(2)}, u32[]{:S(2)}) collective-permute-start(f32[32,128]{1,0:T(8,128)S(1)} %get-tuple-element.21), channel_id=1, source_target_pairs={{0,1},{1,2},{2,3},{3,4},{4,5},{5,6},{6,7},{7,0},{8,9},{9,10},{10,1... | collective-permute-start | bytes 49160 | tf_op jit(solution)/shard_map/ppermute | solution.py:516
  60.2 2.6 %collective-permute-start.3 = (f32[32,128]{1,0:T(8,128)S(1)}, f32[32,128]{1,0:T(8,128)S(1)}, u32[]{:S(2)}, u32[]{:S(2)}) collective-permute-start(f32[32,128]{1,0:T(8,128)S(1)} %get-tuple-element.22), channel_id=1, source_target_pairs={{1,0},{2,1},{3,2},{4,3},{5,4},{6,5},{7,6},{0,7},{9,8},{10,9},{11,1... | collective-permute-start | bytes 49160 | tf_op jit(solution)/shard_map/ppermute | solution.py:517
  62.9 0.0 collective-permute-done
  62.9 0.0 collective-permute-done.1
  62.9 0.0 copy-done
  62.9 0.0 copy-done.1
  62.9 3.1 %inner.1.part_ref = f32[40,32,128]{2,1,0:T(8,128)S(1)} custom-call(f32[2688,128]{1,0:T(8,128)S(1)} %bitcast.4, f32[2,32,128]{2,1,0:T(8,128)S(1)} %pad_maximum_fusion.push_ref, f32[40,32,128]{2,1,0:T(8,128)S(1)} %copy-done, f32[40,32,128]{2,1,0:T(8,128)S(1)} %copy-done.1, f32[3,40,32,128]{3,2,1,0:T(8,128)} %gradient_ref.3), custom_call_target="tpu_custom_call" | custom-call | tf_op jit(solution)/shard_map/inner/pallas_call | solution.py:416
  66.0 0.0 collective-permute-done.2.low_ref
  66.0 0.0 collective-permute-done.3.high_ref
  66.0 1.2 %outer.1 = f32[40,32,128]{2,1,0:T(8,128)} custom-call(f32[40,32,128]{2,1,0:T(8,128)S(1)} %inner.1.part_ref, f32[32,128]{1,0:T(8,128)S(1)} %collective-permute-done.2.low_ref, f32[32,128]{1,0:T(8,128)S(1)} %collective-permute-done.3.high_ref), custom_call_target="tpu_custom_call" | custom-call | tf_op jit(solution)/shard_map/outer/pallas_call | solution.py:453
  (3 shorter events, 0.0 us)
Async XLA Ops:
  0.0 10.1 %copy-start.2 = (f32[20]{0:T(128)S(1)}, f32[20]{0:T(128)}, u32[]{:S(2)}) copy-start(f32[20]{0:T(128)} %mesh_ref.3) | copy-start | bytes 244
  2.1 21.8 %all-to-all-start = ((f32[16,2,40,128]{3,2,1,0:T(8,128)}), f32[16,2,40,128]{3,2,1,0:T(8,128)S(1)}, u32[]{:S(2)}, u32[]{:S(2)}) async-start(f32[16,2,40,128]{3,2,1,0:T(8,128)} %bitcast.1), calls=%async_computation | async-start | bytes 1310720 | tf_op jit(solution)/shard_map/all_to_all | solution.py:503
  33.3 25.5 %all-to-all-start.1 = ((f32[16,168,128]{2,1,0:T(8,128)}), f32[16,168,128]{2,1,0:T(8,128)S(1)}, u32[]{:S(2)}, u32[]{:S(2)}) async-start(f32[16,168,128]{2,1,0:T(8,128)} %get-tuple-element.17), calls=%async_computation.1 | async-start | bytes 2752512 | tf_op jit(solution)/shard_map/all_to_all | solution.py:506
  37.1 25.8 %copy-start = (f32[40,32,128]{2,1,0:T(8,128)S(1)}, f32[40,32,128]{2,1,0:T(8,128)}, u32[]{:S(2)}) copy-start(f32[40,32,128]{2,1,0:T(8,128)} %density_ref.3) | copy-start | bytes 1966084
  37.1 25.8 %copy-start.1 = (f32[40,32,128]{2,1,0:T(8,128)S(1)}, f32[40,32,128]{2,1,0:T(8,128)}, u32[]{:S(2)}) copy-start(f32[40,32,128]{2,1,0:T(8,128)} %rate_ref.1) | copy-start | bytes 1966084
  39.1 23.8 %collective-permute-start = (f32[1,32,128]{2,1,0:T(8,128)S(1)}, f32[1,32,128]{2,1,0:T(8,128)S(1)}, u32[]{:S(2)}, u32[]{:S(2)}) collective-permute-start(f32[1,32,128]{2,1,0:T(8,128)S(1)} %get-tuple-element.23), channel_id=1, source_target_pairs={{0,8},{8,16},{16,24},{24,32},{32,40},{40,48},{48,56},{56,64},{64,7... | collective-permute-start | bytes 49160 | tf_op jit(solution)/shard_map/ppermute | solution.py:511
  39.6 23.3 %collective-permute-start.1 = (f32[1,32,128]{2,1,0:T(8,128)S(1)}, f32[1,32,128]{2,1,0:T(8,128)S(1)}, u32[]{:S(2)}, u32[]{:S(2)}) collective-permute-start(f32[1,32,128]{2,1,0:T(8,128)S(1)} %get-tuple-element.24), channel_id=1, source_target_pairs={{8,0},{16,8},{24,16},{32,24},{40,32},{48,40},{56,48},{64,56},{72,6... | collective-permute-start | bytes 49160 | tf_op jit(solution)/shard_map/ppermute | solution.py:511
  58.8 7.2 %collective-permute-start.2 = (f32[32,128]{1,0:T(8,128)S(1)}, f32[32,128]{1,0:T(8,128)S(1)}, u32[]{:S(2)}, u32[]{:S(2)}) collective-permute-start(f32[32,128]{1,0:T(8,128)S(1)} %get-tuple-element.21), channel_id=1, source_target_pairs={{0,1},{1,2},{2,3},{3,4},{4,5},{5,6},{6,7},{7,0},{8,9},{9,10},{10,1... | collective-permute-start | bytes 49160 | tf_op jit(solution)/shard_map/ppermute | solution.py:516
  60.2 5.8 %collective-permute-start.3 = (f32[32,128]{1,0:T(8,128)S(1)}, f32[32,128]{1,0:T(8,128)S(1)}, u32[]{:S(2)}, u32[]{:S(2)}) collective-permute-start(f32[32,128]{1,0:T(8,128)S(1)} %get-tuple-element.22), channel_id=1, source_target_pairs={{1,0},{2,1},{3,2},{4,3},{5,4},{6,5},{7,6},{0,7},{9,8},{10,9},{11,1... | collective-permute-start | bytes 49160 | tf_op jit(solution)/shard_map/ppermute | solution.py:517
